TPU v7x, 128 devices: a whole 4x4x4 slice. The times are simulated.
128 devices in a mesh: time: 16 (over z, y_lo, core), chan: 8 (over y_hi, x).
Axes of the slice: x: 4, y: 4 (y_hi: 2, y_lo: 2; y = y_hi * 2 + y_lo), z: 4, core: 2. Of those that a mesh axis runs over, the one named last changes fastest.
Arguments:
- fade_rate: float32 [1, 8192, 4096], P(None, 'time', 'chan'), may hold values from 0.2 to 2
- update_in: bfloat16 [1, 8192, 4096], P(None, 'time', 'chan'), may hold values from -6 to 6
- norm_gain: float32 [4096], P('chan'), may hold values from 0.25 to 1.75
Outputs:
- mixed_out: bfloat16 [1, 8192, 4096], P(None, 'time', 'chan')
All inputs are finite; a program needn't handle non-finite values.
Results may differ from a plain program's by a relative error of at most 0.001.
Values sent between devices are 32-bit elements; how exact they have to be, the bound alone decides.
A program may use at most 64 MiB of HBM per device.

v0:
```python
import jax
import jax.numpy as jnp
from jax import lax
from jax.sharding import Mesh
from jax.sharding import PartitionSpec as P

CHAN = ("chan_0", "chan_1")


def entering(value, axis, join, neutral):
    count, mine = (lax.axis_size(axis), lax.axis_index(axis))
    pieces = jax.tree.map(lambda part: lax.all_gather(part, axis), value)
    so_far = jax.tree.map(
        lambda part, zero: jnp.full_like(part, 0) + jnp.asarray(zero, part.dtype), value, neutral
    )

    def entering_step(position, so_far):
        longer = join(so_far, jax.tree.map(lambda part: part[position], pieces))
        return jax.tree.map(lambda new, old: jnp.where(position < mine, new, old), longer, so_far)

    return lax.fori_loop(0, count - 1, entering_step, so_far)


def gathered_once(array, axis):
    leaves = jax.tree.leaves(array)
    sequence = sorted(range(len(leaves)), key=lambda k: -leaves[k].size)
    width = (1, *leaves[sequence[0]].shape)[-1]
    lines = [
        jnp.pad(leaves[k].reshape(-1), (0, -leaves[k].size % width)).reshape(-1, width)
        for k in sequence
    ]
    both, at, found = (lax.all_gather(jnp.concatenate(lines), axis), 0, {})
    for k, line in zip(sequence, lines):
        section = both[:, at : at + len(line)].reshape(len(both), -1)
        found[k] = section[:, : leaves[k].size].reshape(-1, *leaves[k].shape)
        at += len(line)
    numbers = iter(range(len(leaves)))
    return jax.tree.map(lambda _: found[next(numbers)], array)


def carried_in(value, axis, join, neutral):
    count, mine = (lax.axis_size(axis), lax.axis_index(axis))
    pieces = gathered_once(value, axis)
    pieces = jax.tree.map(lambda part: part[::-1], pieces)
    mine = count - 1 - mine
    so_far = jax.tree.map(
        lambda part, zero: jnp.full_like(part, 0) + jnp.asarray(zero, part.dtype), value, neutral
    )

    def carried_step(position, so_far):
        longer = join(so_far, jax.tree.map(lambda part: part[position], pieces))
        return jax.tree.map(lambda new, old: jnp.where(position < mine, new, old), longer, so_far)

    return lax.fori_loop(0, count - 1, carried_step, so_far)


def over_axes(array, axes):
    for axis in axes:
        array = lax.psum(array, axis)
    return array


def join_pair(earlier, later):
    return (earlier[0] * later[0], later[0] * earlier[1] + later[1])


def per_device(fade_rate, update_in, norm_gain):
    total_length = fade_rate.shape[1] * lax.axis_size("time")
    keep = jnp.exp(-fade_rate / total_length)
    push = update_in.astype(jnp.float32) * total_length ** (-0.5)
    product, forward = lax.associative_scan(join_pair, (keep, push), axis=1)
    entering_forward = entering(
        (product[:, -1], forward[:, -1]),
        "time",
        join_pair,
        (jnp.ones_like(keep[:, 0]), jnp.zeros_like(push[:, 0])),
    )
    forward = forward + product * entering_forward[1][:, None]
    product, backward = lax.associative_scan(join_pair, (keep, push), axis=1, reverse=True)
    entering_backward = carried_in(
        (product[:, 0], backward[:, 0]),
        "time",
        join_pair,
        (jnp.ones_like(keep[:, 0]), jnp.zeros_like(push[:, 0])),
    )
    backward = backward + product * entering_backward[1][:, None]
    states = forward + backward
    power = over_axes(jnp.sum(states * states, axis=-1, keepdims=True), CHAN) / (
        states.shape[-1] * lax.axis_size(CHAN)
    )
    mixed_out = (states * lax.rsqrt(power + 1e-06) * norm_gain).astype(jnp.bfloat16)
    return mixed_out


def solution(mesh):
    split = Mesh(mesh.devices.reshape(mesh.shape["time"], 2, 4), ("time", "chan_0", "chan_1"))
    in_specs = (P(None, "time", CHAN), P(None, "time", CHAN), P(CHAN))
    out_specs = P(None, "time", CHAN)
    return jax.shard_map(
        per_device, mesh=split, in_specs=in_specs, out_specs=out_specs, check_vma=False
    )
```

profile of v0, /device:TPU:0, one launch (start us, length us, event | category | flops | bytes accessed | tf_op | source)
XLA Modules:
  0.0 159.9 jit_solution(11750504056960354731)
XLA Ops:
  0.0 1.4 multiply_exponential_fusion
  1.4 0.5 slice.552
  1.9 0.5 slice.548
  2.5 2.7 %slice.639 = f32[1,256,512]{2,1,0:T(8,128)} reverse(f32[1,256,512]{2,1,0:T(8,128)S(1)} %slice.548), dimensions={1} | reverse | bytes 1048576 | tf_op jit(solution)/shard_map/slice | solution.py:79
  5.2 2.7 %slice.635 = f32[1,256,512]{2,1,0:T(8,128)} reverse(f32[1,256,512]{2,1,0:T(8,128)S(1)} %slice.552), dimensions={1} | reverse | bytes 1048576 | tf_op jit(solution)/shard_map/slice | solution.py:79
  7.8 0.5 slice.633
  8.4 2.1 %slice.547 = f32[1,255,512]{2,1,0:T(8,128)} slice(f32[1,512,512]{2,1,0:T(8,128)S(1)} %multiply_exponential_fusion), slice={[0:1:1], [2:512:2], [0:512:1]} | slice | bytes 1044480 | tf_op jit(solution)/shard_map/slice | solution.py:71
  10.5 2.8 %slice.634 = f32[1,255,512]{2,1,0:T(8,128)} reverse(f32[1,255,512]{2,1,0:T(8,128)S(1)} %slice.633), dimensions={1} | reverse | bytes 1044480 | tf_op jit(solution)/shard_map/slice | solution.py:79
  13.5 2.1 %slice.612 = f32[1,255,512]{2,1,0:T(8,128)} slice(f32[1,512,512]{2,1,0:T(8,128)S(1)} %broadcast_multiply_fusion.1), slice={[0:1:1], [2:512:2], [0:512:1]} | slice | bytes 1044480 | tf_op jit(solution)/shard_map/slice | solution.py:71
  15.6 0.5 slice.550
  16.1 0.5 slice.549
  16.9 0.3 slice.610
  17.3 0.3 slice.556
  18.3 0.3 slice.554
  18.7 0.3 slice.553
  22.6 0.9 copy-done.12
  23.7 0.4 fusion.1
  24.0 0.9 add.464
  24.9 0.9 add.454
  26.2 2.3 %pad.237 = f32[1,512,512]{2,1,0:T(8,128)S(1)} pad(f32[1,256,512]{2,1,0:T(8,128)} %add.454, f32[]{:T(128)} %constant.60.clone.1), padding=0_0_0x1_0_1x0_0_0 | pad | bytes 1572868 | tf_op jit(solution)/shard_map/pad | solution.py:71
  28.6 21.2 %all_gather.13 = f32[16,1,512]{2,1,0:T(1,128)S(1)} all-gather(f32[1,1,512]{2,1,0:T(1,128)S(1)} %slice_add_fusion.2), channel_id=1, replica_groups=mesh['time'=16,'chan_0'=2,'chan_1'=4] {'time'}, dimensions={0}, use_global_device_ids=true | all-gather | bytes 34816 | tf_op jit(solution)/shard_map/all_gather | solution.py:12
  49.8 4.7 %pad.255 = f32[1,512,512]{2,1,0:T(8,128)} pad(f32[1,256,512]{2,1,0:T(8,128)} %add.464, f32[]{:T(128)} %constant.60.clone.1), padding=0_0_0x1_0_1x0_0_0 | pad | bytes 1572868 | tf_op jit(solution)/shard_map/pad | solution.py:71
  54.4 0.7 slice_add_fusion.3
  55.2 16.5 %all_gather.12 = f32[16,1,512]{2,1,0:T(1,128)S(1)} all-gather(f32[1,1,512]{2,1,0:T(1,128)S(1)} %slice_add_fusion.3), channel_id=1, replica_groups=mesh['time'=16,'chan_0'=2,'chan_1'=4] {'time'}, dimensions={0}, use_global_device_ids=true | all-gather | bytes 34816 | tf_op jit(solution)/shard_map/all_gather | solution.py:12
  71.7 0.6 while.28
  72.3 6.3 %reverse.9 = f32[1,512,512]{2,1,0:T(8,128)S(1)} reverse(bf16[1,512,512]{2,1,0:T(8,128)(2,1)} %param.8), dimensions={1} | reverse | bytes 1572864 | tf_op jit(solution)/shard_map/reverse
  78.8 2.1 %slice.699 = f32[1,255,512]{2,1,0:T(8,128)} slice(f32[1,512,512]{2,1,0:T(8,128)S(1)} %broadcast_multiply_fusion), slice={[0:1:1], [2:512:2], [0:512:1]} | slice | bytes 1044480 | tf_op jit(solution)/shard_map/slice | solution.py:79
  80.9 2.1 %slice.637 = f32[1,256,512]{2,1,0:T(8,128)} slice(f32[1,512,512]{2,1,0:T(8,128)S(1)} %broadcast_multiply_fusion), slice={[0:1:1], [1:512:2], [0:512:1]} | slice | bytes 1048576 | tf_op jit(solution)/shard_map/slice | solution.py:79
  82.9 2.1 %slice.636 = f32[1,256,512]{2,1,0:T(8,128)} slice(f32[1,512,512]{2,1,0:T(8,128)S(1)} %broadcast_multiply_fusion), slice={[0:1:1], [0:511:2], [0:512:1]} | slice | bytes 1048576 | tf_op jit(solution)/shard_map/slice | solution.py:79
  85.0 1.4 fusion.23
  87.1 0.3 slice.640
  87.5 0.3 slice.697
  92.1 0.9 copy-done.13
  93.2 0.4 add_multiply_fusion
  93.5 0.9 add.490
  94.4 0.9 add.500
  95.7 2.1 %pad.291 = f32[1,512,512]{2,1,0:T(8,128)S(1)} pad(f32[1,256,512]{2,1,0:T(8,128)} %add.500, f32[]{:T(128)} %constant.60.clone.1), padding=0_0_0x1_0_1x0_0_0 | pad | bytes 1572868 | tf_op jit(solution)/shard_map/pad | solution.py:79
  97.8 1.2 add.501
  99.0 8.9 %rev.18 = f32[1,512,512]{2,1,0:T(8,128)} reverse(f32[1,512,512]{2,1,0:T(8,128)} %add.501), dimensions={1} | reverse | bytes 2097152 | tf_op jit(solution)/shard_map/rev | solution.py:79
  108.1 1.2 add.492
  109.3 9.1 %rev.17 = f32[1,512,512]{2,1,0:T(8,128)} reverse(f32[1,512,512]{2,1,0:T(8,128)} %add.492), dimensions={1} | reverse | bytes 2097152 | tf_op jit(solution)/shard_map/rev | solution.py:79
  118.4 17.9 %all-gather.1 = f32[16,2,512]{2,1,0:T(2,128)S(1)} all-gather(f32[1,2,512]{2,1,0:T(2,128)S(1)} %maximum_bitcast_fusion), channel_id=2, replica_groups=mesh['time'=16,'chan_0'=2,'chan_1'=4] {'time'}, dimensions={0}, use_global_device_ids=true | all-gather | bytes 69632 | tf_op jit(solution)/shard_map/all_gather | solution.py:32
  136.4 0.6 while.29
  137.0 3.1 %multiply_reduce_fusion = (f32[512]{0:T(512)S(1)}, f32[1,512,512]{2,1,0:T(8,128)}) fusion(f32[1,512,512]{2,1,0:T(8,128)} %rev.17, f32[1,512,512]{2,1,0:T(8,128)} %rev.18, f32[512]{0:T(512)S(1)} %bitcast.34, f32[512]{0:T(512)S(1)} %bitcast.35, f32[1,512,512]{2,1,0:T(8,128)S(1)} %copy-done.1, f32[1,512,512]{2,1,0:T(8,128)} %pad.255, ...), kind=kLoop, calls=%fused_computation.9 | loop fusion | flops 2358784 | bytes 7346176 | tf_op jit(solution)/shard_map/reduce_sum | solution.py:88
  140.2 6.4 %psum.14 = f32[1,512,1]{1,2,0:T(1,128)S(1)} all-reduce(f32[1,512,1]{1,2,0:T(1,128)S(1)} %bitcast.37), channel_id=1, replica_groups=mesh['time'=16,'chan_0'=2,'chan_1'=4] {'chan_0'}, use_global_device_ids=true, to_apply=%region_5.6 | all-reduce | flops 512 | bytes 4096 | tf_op jit(solution)/shard_map/psum | solution.py:59
  146.6 10.5 %psum.15 = f32[1,512,1]{1,2,0:T(1,128)S(1)} all-reduce(f32[1,512,1]{1,2,0:T(1,128)S(1)} %psum.14), channel_id=1, replica_groups=mesh['time'=16,'chan_0'=2,'chan_1'=4] {'chan_1'}, use_global_device_ids=true, to_apply=%region_6.7 | all-reduce | flops 512 | bytes 4096 | tf_op jit(solution)/shard_map/psum | solution.py:59
  157.1 0.7 copy-done.14
  157.7 2.2 %multiply_convert_fusion = bf16[1,512,512]{2,1,0:T(8,128)(2,1)} fusion(f32[1,512,512]{2,1,0:T(8,128)} %get-tuple-element.252, f32[512]{0:T(512)S(1)} %copy-done.14, f32[512]{0:T(512)S(1)} %bitcast.36), kind=kLoop, calls=%fused_computation.8 | loop fusion | flops 786432 | bytes 1576960 | tf_op jit(solution)/shard_map/convert_element_type | solution.py:91
  (318 shorter events, 10.5 us)
Async XLA Ops:
  10.5 2.8 %copy-start.6 = (bf16[1,512,512]{2,1,0:T(8,128)(2,1)S(1)}, bf16[1,512,512]{2,1,0:T(8,128)(2,1)}, u32[]{:S(2)}) copy-start(bf16[1,512,512]{2,1,0:T(8,128)(2,1)} %param.8) | copy-start | bytes 1572868
  22.4 1.0 copy-start.12
  22.5 1.1 copy-start.11
  26.1 28.4 %copy-start = (f32[1,512,512]{2,1,0:T(8,128)}, f32[1,512,512]{2,1,0:T(8,128)S(1)}, u32[]{:S(2)}) copy-start(f32[1,512,512]{2,1,0:T(8,128)S(1)} %pad.254) | copy-start | bytes 3145732
  26.2 28.2 %copy-start.2 = (f32[1,512,512]{2,1,0:T(8,128)}, f32[1,512,512]{2,1,0:T(8,128)S(1)}, u32[]{:S(2)}) copy-start(f32[1,512,512]{2,1,0:T(8,128)S(1)} %pad.236) | copy-start | bytes 3145732
  28.6 50.1 %copy-start.4 = (f32[1,512,512]{2,1,0:T(8,128)}, f32[1,512,512]{2,1,0:T(8,128)S(1)}, u32[]{:S(2)}) copy-start(f32[1,512,512]{2,1,0:T(8,128)S(1)} %pad.237) | copy-start | bytes 3145732
  82.9 2.1 %copy-start.8 = (f32[1,256,512]{2,1,0:T(8,128)S(1)}, f32[1,256,512]{2,1,0:T(8,128)}, u32[]{:S(2)}) copy-start(f32[1,256,512]{2,1,0:T(8,128)} %slice.639) | copy-start | bytes 1572868
  82.9 2.1 %copy-start.9 = (f32[1,256,512]{2,1,0:T(8,128)S(1)}, f32[1,256,512]{2,1,0:T(8,128)}, u32[]{:S(2)}) copy-start(f32[1,256,512]{2,1,0:T(8,128)} %slice.635) | copy-start | bytes 1572868
  92.0 1.0 copy-start.13
  92.0 1.1 copy-start.10
  99.0 8.9 %copy-start.7 = (f32[1,256,512]{2,1,0:T(8,128)S(1)}, f32[1,256,512]{2,1,0:T(8,128)}, u32[]{:S(2)}) copy-start(f32[1,256,512]{2,1,0:T(8,128)} %add.490) | copy-start | bytes 1572868
  108.1 28.9 %copy-start.5 = (f32[1,512,512]{2,1,0:T(8,128)S(1)}, f32[1,512,512]{2,1,0:T(8,128)}, u32[]{:S(2)}) copy-start(f32[1,512,512]{2,1,0:T(8,128)} %copy-done.4) | copy-start | bytes 3145732
  109.3 27.7 %copy-start.1 = (f32[1,512,512]{2,1,0:T(8,128)S(1)}, f32[1,512,512]{2,1,0:T(8,128)}, u32[]{:S(2)}) copy-start(f32[1,512,512]{2,1,0:T(8,128)} %copy-done) | copy-start | bytes 3145732
  109.3 27.7 %copy-start.3 = (f32[1,512,512]{2,1,0:T(8,128)S(1)}, f32[1,512,512]{2,1,0:T(8,128)}, u32[]{:S(2)}) copy-start(f32[1,512,512]{2,1,0:T(8,128)} %copy-done.2) | copy-start | bytes 3145732
  157.0 0.7 copy-start.14
where the time goes:
time: 162 us; the launch traced here: 160 us
  blocking collectives  72.5 us (45%)
  local copies, waits for them, and re-layouts  66.5 us (41%)
  other arithmetic  18.4 us (11%)
  between operations  1.76 us (1%)
    all_gather x2, blocking collectives, entering(): pieces = jax.tree.map(lambda part: lax.all_gather(part, axis), value)  37.7 us
    slice x60, local copies, waits for them, and re-layouts, per_device(): lax.associative_scan(join_pair, (keep, push), axis=1, reverse=True)  18.4 us
    rev x2, local copies, waits for them, and re-layouts, per_device(): lax.associative_scan(join_pair, (keep, push), axis=1, reverse=True)  18 us
    all_gather x1, blocking collectives, gathered_once(): both, at, found = (lax.all_gather(jnp.concatenate(lines), axis), 0, {})  17.9 us
    psum x2, blocking collectives, over_axes(): array = lax.psum(array, axis)  16.9 us
    slice x60, local copies, waits for them, and re-layouts, per_device(): product, forward = lax.associative_scan(join_pair, (keep, push), axis=1)  9.83 us
    pad x32, local copies, waits for them, and re-layouts, per_device(): product, forward = lax.associative_scan(join_pair, (keep, push), axis=1)  7.96 us
    another operation x1, local copies, waits for them, and re-layouts  6.26 us

commit v1 on v0

v1 whole, which is shorter than its diff:
```python
import functools

import jax
import jax.numpy as jnp
from jax import lax
from jax.experimental import pallas as pl
from jax.experimental.pallas import tpu as pltpu
from jax.sharding import PartitionSpec as P

MESH = pl.DeviceIdType.MESH
LANES = 128
F32 = jnp.float32
BF16 = jnp.bfloat16


def ring_gap(step, size):
    return min(step, size - step)


def time_peers():
    offsets = [(z, y, c) for z in range(4) for y in range(2) for c in range(2)][1:]
    return sorted(offsets, key=lambda o: -(4 * ring_gap(o[0], 4) + 4 * o[1] + o[2]))


def chan_peers():
    offsets = [(y, x) for y in range(2) for x in range(4)][1:]
    return sorted(offsets, key=lambda o: -(2 * o[0] + ring_gap(o[1], 4)))


def split(value):
    high = value.astype(BF16)
    return high, (value - high.astype(F32)).astype(BF16)


def prefix(lower, value):
    block = lower.shape[0]
    carry, parts = None, []
    for start in range(0, value.shape[0], block):
        high, low = split(value[start : start + block])
        part = jnp.dot(lower, high, preferred_element_type=F32)
        part = part + jnp.dot(lower, low, preferred_element_type=F32)
        if carry is not None:
            part = part + carry
        carry = part[block - 1 : block]
        parts.append(part)
    return jnp.concatenate(parts, axis=0)


def kernel(
    sizes,
    fade_hbm,
    update_hbm,
    gain_ref,
    out_ref,
    fade,
    update,
    own,
    through,
    near,
    leave,
    message,
    inbox,
    powers,
    load_sem,
    sent_sem,
    inbox_sem,
    power_sent_sem,
    power_sem,
):
    n_time, n_chan = sizes
    rows, columns = fade.shape
    length = rows * n_time
    channels = columns * n_chan
    groups = columns // LANES
    me_t, me_c = lax.axis_index("time"), lax.axis_index("chan")

    loads = [
        pltpu.make_async_copy(fade_hbm.at[0], fade, load_sem.at[0]),
        pltpu.make_async_copy(update_hbm.at[0], update, load_sem.at[1]),
    ]
    for load in loads:
        load.start()

    z, y, core = me_t // 4, (me_t // 2) % 2, me_t % 2
    later_times = [
        ((z + dz) % 4) * 4 + ((y + dy) % 2) * 2 + (core + dc) % 2 for dz, dy, dc in time_peers()
    ]
    cy, cx = me_c // 4, me_c % 4
    other_chans = [((cy + dy) % 2) * 4 + (cx + dx) % 4 for dy, dx in chan_peers()]

    barrier = pltpu.get_barrier_semaphore()
    for peer in other_chans:
        pl.semaphore_signal(barrier, inc=1, device_id=(me_t, peer), device_id_type=MESH)
    for peer in later_times:
        pl.semaphore_signal(barrier, inc=1, device_id=(peer, me_c), device_id_type=MESH)

    half = rows // 2
    lower = (
        lax.broadcasted_iota(jnp.int32, (half, half), 0)
        >= lax.broadcasted_iota(jnp.int32, (half, half), 1)
    ).astype(BF16)

    for load in loads:
        load.wait()

    for g in range(groups):
        at = slice(g * LANES, (g + 1) * LANES)
        rate = fade[:, at] * (1.0 / length)
        push = update[:, at].astype(F32) * length**-0.5
        total = prefix(lower, rate)
        last = total[rows - 1 :]
        down = jnp.exp(-total)
        up = jnp.exp(total)
        before = total - rate
        grown = up * push
        shrunk = jnp.exp(-before) * push
        whole = jnp.exp(-last)
        message[0, 0, g : g + 1] = whole
        message[1, 0, g : g + 1] = whole
        message[0, 1, g : g + 1] = whole * jnp.sum(grown, axis=0, keepdims=True)
        message[1, 1, g : g + 1] = jnp.sum(shrunk, axis=0, keepdims=True)
        through[:, at] = down
        near[:, at] = before
        own[:, at] = grown
        leave[:, at] = shrunk

    pl.semaphore_wait(barrier, len(later_times) + len(other_chans))
    sends = []
    for peer in later_times:
        sends.append(
            pltpu.make_async_remote_copy(
                src_ref=message.at[jnp.where(peer > me_t, 0, 1)],
                dst_ref=inbox.at[me_t],
                send_sem=sent_sem,
                recv_sem=inbox_sem,
                device_id=(peer, me_c),
                device_id_type=MESH,
            )
        )
        sends[-1].start()

    for g in range(groups):
        at = slice(g * LANES, (g + 1) * LANES)
        grown, shrunk = own[:, at], leave[:, at]
        before = near[:, at]
        back = jnp.exp(before)
        ahead = jnp.sum(shrunk, axis=0, keepdims=True) - prefix(lower, shrunk) + shrunk
        own[:, at] = through[:, at] * prefix(lower, grown) + back * ahead
        near[:, at] = back * message[0, 0, g : g + 1]

    inbox[me_t] = message[0]
    pltpu.make_async_copy(
        inbox.at[pl.ds(0, n_time - 1)], inbox.at[pl.ds(0, n_time - 1)], inbox_sem
    ).wait()

    earlier = jnp.zeros((groups, LANES), F32)
    for k in range(n_time - 1):
        earlier = jnp.where(k < me_t, earlier * inbox[k, 0] + inbox[k, 1], earlier)
    later = jnp.zeros((groups, LANES), F32)
    for k in range(n_time - 1, 0, -1):
        later = jnp.where(k > me_t, later * inbox[k, 0] + inbox[k, 1], later)

    for b in range(rows // LANES):
        block = slice(b * LANES, (b + 1) * LANES)
        squares = None
        for g in range(groups):
            at = slice(g * LANES, (g + 1) * LANES)
            states = (
                own[block, at]
                + through[block, at] * earlier[g : g + 1]
                + near[block, at] * later[g : g + 1]
            )
            own[block, at] = states
            square = states * states
            squares = square if squares is None else squares + square
        powers[me_c, b : b + 1] = jnp.sum(squares.T, axis=0, keepdims=True)

    for peer in other_chans:
        sends.append(
            pltpu.make_async_remote_copy(
                src_ref=powers.at[me_c],
                dst_ref=powers.at[me_c],
                send_sem=power_sent_sem,
                recv_sem=power_sem,
                device_id=(me_t, peer),
                device_id_type=MESH,
            )
        )
        sends[-1].start()
    pltpu.make_async_copy(
        powers.at[pl.ds(0, n_chan - 1)], powers.at[pl.ds(0, n_chan - 1)], power_sem
    ).wait()

    power = powers[0]
    for k in range(1, n_chan):
        power = power + powers[k]
    scale = lax.rsqrt(power * (1.0 / channels) + 1e-06)
    for b in range(rows // LANES):
        block = slice(b * LANES, (b + 1) * LANES)
        by_row = jnp.broadcast_to(scale[b : b + 1], (LANES, LANES)).T
        for g in range(groups):
            at = slice(g * LANES, (g + 1) * LANES)
            out_ref[0, block, at] = (own[block, at] * by_row * gain_ref[:, at]).astype(BF16)

    pltpu.make_async_copy(
        inbox.at[pl.ds(0, n_time - 1)], inbox.at[pl.ds(0, n_time - 1)], sent_sem
    ).wait()
    pltpu.make_async_copy(
        powers.at[pl.ds(0, n_chan - 1)], powers.at[pl.ds(0, n_chan - 1)], power_sent_sem
    ).wait()


def per_device(fade_rate, update_in, norm_gain):
    n_time, n_chan = lax.axis_size("time"), lax.axis_size("chan")
    _, rows, columns = fade_rate.shape
    groups = columns // LANES
    return pl.pallas_call(
        functools.partial(kernel, (n_time, n_chan)),
        out_shape=jax.ShapeDtypeStruct((1, rows, columns), BF16),
        in_specs=[
            pl.BlockSpec(memory_space=pl.ANY),
            pl.BlockSpec(memory_space=pl.ANY),
            pl.BlockSpec(memory_space=pltpu.VMEM),
        ],
        out_specs=pl.BlockSpec(memory_space=pltpu.VMEM),
        scratch_shapes=[
            pltpu.VMEM((rows, columns), F32),
            pltpu.VMEM((rows, columns), BF16),
            pltpu.VMEM((rows, columns), F32),
            pltpu.VMEM((rows, columns), F32),
            pltpu.VMEM((rows, columns), F32),
            pltpu.VMEM((rows, columns), F32),
            pltpu.VMEM((2, 2, groups, LANES), F32),
            pltpu.VMEM((n_time, 2, groups, LANES), F32),
            pltpu.VMEM((n_chan, rows // LANES, LANES), F32),
            pltpu.SemaphoreType.DMA((2,)),
            pltpu.SemaphoreType.DMA,
            pltpu.SemaphoreType.DMA,
            pltpu.SemaphoreType.DMA,
            pltpu.SemaphoreType.DMA,
        ],
        compiler_params=pltpu.CompilerParams(collective_id=0, has_side_effects=True),
        name="filter_norm",
    )(fade_rate, update_in, norm_gain.reshape(1, columns))


def solution(mesh):
    return jax.shard_map(
        per_device,
        mesh=mesh,
        in_specs=(P(None, "time", "chan"), P(None, "time", "chan"), P("chan")),
        out_specs=P(None, "time", "chan"),
        check_vma=False,
    )
```

time: 162 us -> 21.5 us (0.13); the launches traced: 160 us -> 21.3 us
  blocking collectives: 72.5 us -> 0 us
  local copies, waits for them, and re-layouts: 66.5 us -> 1.87 us
  Pallas kernels: 0 us -> 19.4 us
  other arithmetic: 18.4 us -> 0 us
  between operations: 1.76 us -> 0.01 us
    all_gather x3 -> x0, blocking collectives: 55.6 us -> none  [the longest x2 37.7 us: entering(): pieces = jax.tree.map(lambda part: lax.all_gather(part, axis), value)]
    slice x121 -> x0, local copies, waits for them, and re-layouts: 28.2 us -> none  [the longest x60 18.4 us: per_device(): lax.associative_scan(join_pair, (keep, push), axis=1, reverse=True)]
    pallas_call x0 -> x1, Pallas kernels: none -> 19.4 us  [per_device(): pl.pallas_call(functools.partial(kernel, (n_time, n_chan)), out_shape=jax...]
    rev x4 -> x0, local copies, waits for them, and re-layouts: 18.1 us -> none  [the longest x2 18 us: per_device(): lax.associative_scan(join_pair, (keep, push), axis=1, reverse=True)]
    psum x2 -> x0, blocking collectives: 16.9 us -> none  [over_axes(): array = lax.psum(array, axis)]
    pad x64 -> x0, local copies, waits for them, and re-layouts: 11.2 us -> none  [the longest x32 7.96 us: per_device(): product, forward = lax.associative_scan(join_pair, (keep, push), axis=1)]
    add x49 -> x0, other arithmetic: 8.05 us -> none  [the longest x17 4.32 us: per_device(): lax.associative_scan(join_pair, (keep, push), axis=1, reverse=True)]
    another operation x1 -> x0, local copies, waits for them, and re-layouts: 6.26 us -> none
where the time goes in v1:
time: 21.5 us; the launch traced here: 21.3 us
  Pallas kernels  19.4 us (90%)
  local copies, waits for them, and re-layouts  1.87 us (9%)
    pallas_call x1, Pallas kernels, per_device(): pl.pallas_call(functools.partial(kernel, (n_time, n_chan)), out_shape=jax...  19.4 us
    unnamed x1, local copies, waits for them, and re-layouts  1.87 us

profile of v1, /device:TPU:0, one launch (start us, length us, event | category | flops | bytes accessed | tf_op | source)
XLA Modules:
  0.0 21.3 jit_solution(9244745929798221803)
XLA Ops:
  0.0 19.4 %filter_norm.1 = bf16[1,512,512]{2,1,0:T(8,128)(2,1)} custom-call(f32[1,512,512]{2,1,0:T(8,128)} %fade_hbm.1, bf16[1,512,512]{2,1,0:T(8,128)(2,1)} %update_hbm.1, f32[1,512]{1,0:T(1,128)} %bitcast.1), custom_call_target="tpu_custom_call" | custom-call | tf_op jit(solution)/shard_map/filter_norm/pallas_call | solution.py:217
  19.4 1.9 %copy.5 = bf16[1,512,512]{2,1,0:T(8,128)(2,1)} copy(bf16[1,512,512]{2,1,0:T(8,128)(2,1)} %filter_norm.1) | data formatting | bytes 1048576

commit v2 on v1

--- a/solution.py
+++ b/solution.py
@@ -9,6 +9,8 @@
 
 MESH = pl.DeviceIdType.MESH
 LANES = 128
+PITCH = 9
+LOG2E = 1.4426950408889634
 F32 = jnp.float32
 BF16 = jnp.bfloat16
 
@@ -57,7 +59,9 @@
     own,
     through,
     near,
-    leave,
+    keeps,
+    pushes,
+    lower,
     message,
     inbox,
     powers,
@@ -68,18 +72,23 @@
     power_sem,
 ):
     n_time, n_chan = sizes
-    rows, columns = fade.shape
+    groups, rows, _ = fade.shape
+    columns = groups * LANES
     length = rows * n_time
     channels = columns * n_chan
-    groups = columns // LANES
     me_t, me_c = lax.axis_index("time"), lax.axis_index("chan")
 
-    loads = [
-        pltpu.make_async_copy(fade_hbm.at[0], fade, load_sem.at[0]),
-        pltpu.make_async_copy(update_hbm.at[0], update, load_sem.at[1]),
-    ]
-    for load in loads:
-        load.start()
+    loads = []
+    for g in range(groups):
+        at = pl.ds(g * LANES, LANES)
+        loads.append(
+            (
+                pltpu.make_async_copy(fade_hbm.at[0, :, at], fade.at[g], load_sem.at[0, g]),
+                pltpu.make_async_copy(update_hbm.at[0, :, at], update.at[g], load_sem.at[1, g]),
+            )
+        )
+        for load in loads[g]:
+            load.start()
 
     z, y, core = me_t // 4, (me_t // 2) % 2, me_t % 2
     later_times = [
@@ -95,34 +104,49 @@
         pl.semaphore_signal(barrier, inc=1, device_id=(peer, me_c), device_id_type=MESH)
 
     half = rows // 2
-    lower = (
-        lax.broadcasted_iota(jnp.int32, (half, half), 0)
-        >= lax.broadcasted_iota(jnp.int32, (half, half), 1)
-    ).astype(BF16)
-
-    for load in loads:
-        load.wait()
+    steps = half // 8
 
     for g in range(groups):
-        at = slice(g * LANES, (g + 1) * LANES)
-        rate = fade[:, at] * (1.0 / length)
-        push = update[:, at].astype(F32) * length**-0.5
-        total = prefix(lower, rate)
-        last = total[rows - 1 :]
-        down = jnp.exp(-total)
-        up = jnp.exp(total)
-        before = total - rate
-        grown = up * push
-        shrunk = jnp.exp(-before) * push
-        whole = jnp.exp(-last)
+        for load in loads[g]:
+            load.wait()
+        ends = []
+        summed = None
+        for h in range(2):
+            slab = 2 * g + h
+            for i in range(0, half, 16):
+                at = pl.ds(h * half + i, 16)
+                rate = fade[g, at]
+                keep = jnp.exp2(rate * (-LOG2E / length))
+                push = update[g, at].astype(F32)
+                for q in range(2):
+                    run, step = divmod(i + 8 * q, steps)
+                    to = pl.ds(step * PITCH + run, 8, stride=PITCH)
+                    keeps[slab, to] = keep[8 * q : 8 * q + 8]
+                    pushes[slab, to] = push[8 * q : 8 * q + 8]
+                    part = rate[8 * q : 8 * q + 8]
+                    summed = part if summed is None else summed + part
+            weight = keeps[slab, pl.ds(0, 8)]
+            ahead = behind = pushes[slab, pl.ds(0, 8)]
+            for step in range(1, steps):
+                keep = keeps[slab, pl.ds(step * PITCH, 8)]
+                push = pushes[slab, pl.ds(step * PITCH, 8)]
+                ahead = keep * ahead + push
+                behind = behind + weight * push
+                weight = weight * keep
+            for gap in (1, 2, 4):
+                weight_next, ahead_next, behind_next = (
+                    pltpu.roll(x, 8 - gap, 0) for x in (weight, ahead, behind)
+                )
+                behind = behind + weight * behind_next
+                ahead = ahead_next + weight_next * ahead
+                weight = weight * weight_next
+            ends.append((weight[:1], ahead[:1], behind[:1]))
+        (weight_0, ahead_0, behind_0), (weight_1, ahead_1, behind_1) = ends
+        whole = jnp.exp2(jnp.sum(summed, axis=0, keepdims=True) * (-LOG2E / length))
         message[0, 0, g : g + 1] = whole
         message[1, 0, g : g + 1] = whole
-        message[0, 1, g : g + 1] = whole * jnp.sum(grown, axis=0, keepdims=True)
-        message[1, 1, g : g + 1] = jnp.sum(shrunk, axis=0, keepdims=True)
-        through[:, at] = down
-        near[:, at] = before
-        own[:, at] = grown
-        leave[:, at] = shrunk
+        message[0, 1, g : g + 1] = (ahead_1 + weight_1 * ahead_0) * length**-0.5
+        message[1, 1, g : g + 1] = (behind_0 + weight_0 * behind_1) * length**-0.5
 
     pl.semaphore_wait(barrier, len(later_times) + len(other_chans))
     sends = []
@@ -139,14 +163,25 @@
         )
         sends[-1].start()
 
-    for g in range(groups):
-        at = slice(g * LANES, (g + 1) * LANES)
-        grown, shrunk = own[:, at], leave[:, at]
-        before = near[:, at]
+    lower[...] = (
+        lax.broadcasted_iota(jnp.int32, (half, half), 0)
+        >= lax.broadcasted_iota(jnp.int32, (half, half), 1)
+    ).astype(BF16)
+
+    @pl.loop(0, groups)
+    def _(g):
+        rate = fade[g] * (1.0 / length)
+        push = update[g].astype(F32) * length**-0.5
+        total = prefix(lower[...], rate)
+        before = total - rate
+        down = jnp.exp(-total)
         back = jnp.exp(before)
-        ahead = jnp.sum(shrunk, axis=0, keepdims=True) - prefix(lower, shrunk) + shrunk
-        own[:, at] = through[:, at] * prefix(lower, grown) + back * ahead
-        near[:, at] = back * message[0, 0, g : g + 1]
+        grown = jnp.exp(total) * push
+        shrunk = jnp.exp(-before) * push
+        ahead = jnp.sum(shrunk, axis=0, keepdims=True) - prefix(lower[...], shrunk) + shrunk
+        own[g] = down * prefix(lower[...], grown) + back * ahead
+        through[g] = down
+        near[g] = back * down[rows - 1 :]
 
     inbox[me_t] = message[0]
     pltpu.make_async_copy(
@@ -164,13 +199,12 @@
         block = slice(b * LANES, (b + 1) * LANES)
         squares = None
         for g in range(groups):
-            at = slice(g * LANES, (g + 1) * LANES)
             states = (
-                own[block, at]
-                + through[block, at] * earlier[g : g + 1]
-                + near[block, at] * later[g : g + 1]
-            )
-            own[block, at] = states
+                own[g, block]
+                + through[g, block] * earlier[g : g + 1]
+                + near[g, block] * later[g : g + 1]
+            )
+            own[g, block] = states
             square = states * states
             squares = square if squares is None else squares + square
         powers[me_c, b : b + 1] = jnp.sum(squares.T, axis=0, keepdims=True)
@@ -200,7 +234,7 @@
         by_row = jnp.broadcast_to(scale[b : b + 1], (LANES, LANES)).T
         for g in range(groups):
             at = slice(g * LANES, (g + 1) * LANES)
-            out_ref[0, block, at] = (own[block, at] * by_row * gain_ref[:, at]).astype(BF16)
+            out_ref[0, block, at] = (own[g, block] * by_row * gain_ref[:, at]).astype(BF16)
 
     pltpu.make_async_copy(
         inbox.at[pl.ds(0, n_time - 1)], inbox.at[pl.ds(0, n_time - 1)], sent_sem
@@ -216,7 +250,7 @@
     groups = columns // LANES
     return pl.pallas_call(
         functools.partial(kernel, (n_time, n_chan)),
-        out_shape=jax.ShapeDtypeStruct((1, rows, columns), BF16),
+        out_shape=pltpu.VMEM((1, rows, columns), BF16),
         in_specs=[
             pl.BlockSpec(memory_space=pl.ANY),
             pl.BlockSpec(memory_space=pl.ANY),
@@ -224,16 +258,18 @@
         ],
         out_specs=pl.BlockSpec(memory_space=pltpu.VMEM),
         scratch_shapes=[
-            pltpu.VMEM((rows, columns), F32),
-            pltpu.VMEM((rows, columns), BF16),
-            pltpu.VMEM((rows, columns), F32),
-            pltpu.VMEM((rows, columns), F32),
-            pltpu.VMEM((rows, columns), F32),
-            pltpu.VMEM((rows, columns), F32),
+            pltpu.VMEM((groups, rows, LANES), F32),
+            pltpu.VMEM((groups, rows, LANES), BF16),
+            pltpu.VMEM((groups, rows, LANES), F32),
+            pltpu.VMEM((groups, rows, LANES), F32),
+            pltpu.VMEM((groups, rows, LANES), F32),
+            pltpu.VMEM((2 * groups, rows // 16 * PITCH, LANES), F32),
+            pltpu.VMEM((2 * groups, rows // 16 * PITCH, LANES), F32),
+            pltpu.VMEM((rows // 2, rows // 2), BF16),
             pltpu.VMEM((2, 2, groups, LANES), F32),
             pltpu.VMEM((n_time, 2, groups, LANES), F32),
             pltpu.VMEM((n_chan, rows // LANES, LANES), F32),
-            pltpu.SemaphoreType.DMA((2,)),
+            pltpu.SemaphoreType.DMA((2, groups)),
             pltpu.SemaphoreType.DMA,
             pltpu.SemaphoreType.DMA,
             pltpu.SemaphoreType.DMA,

time: 21.5 us -> 18 us (0.84)
  Pallas kernels: 19.4 us -> 17 us
  local copies, waits for them, and re-layouts: 1.87 us -> 0.8 us
    pallas_call x1, Pallas kernels: 19.4 us -> 17 us  [per_device(): pl.pallas_call(functools.partial(kernel, (n_time, n_chan)), out_shape=plt...]
    unnamed x1, local copies, waits for them, and re-layouts: 1.87 us -> 0.8 us
where the time goes in v2:
time: 18 us; the launch traced here: 17.8 us
  Pallas kernels  17 us (94%)
  local copies, waits for them, and re-layouts  0.8 us (4%)
    pallas_call x1, Pallas kernels, per_device(): pl.pallas_call(functools.partial(kernel, (n_time, n_chan)), out_shape=plt...  17 us
    unnamed x1, local copies, waits for them, and re-layouts  0.8 us

profile of v2, /device:TPU:0, one launch (start us, length us, event | category | flops | bytes accessed | tf_op | source)
XLA Modules:
  0.0 17.8 jit_solution(17496068119338799049)
XLA Ops:
  0.0 17.0 %filter_norm.1 = bf16[1,512,512]{2,1,0:T(8,128)(2,1)S(1)} custom-call(f32[1,512,512]{2,1,0:T(8,128)} %fade_hbm.1, bf16[1,512,512]{2,1,0:T(8,128)(2,1)} %update_hbm.1, f32[1,512]{1,0:T(1,128)} %bitcast.1), custom_call_target="tpu_custom_call" | custom-call | tf_op jit(solution)/shard_map/filter_norm/pallas_call | solution.py:251
  17.0 0.8 %copy.5 = bf16[1,512,512]{2,1,0:T(8,128)(2,1)} copy(bf16[1,512,512]{2,1,0:T(8,128)(2,1)S(1)} %filter_norm.1) | data formatting | bytes 1048576

commit v3 on v2

v3 whole, which is shorter than its diff:
```python
import functools

import jax
import jax.numpy as jnp
from jax import lax
from jax.experimental import pallas as pl
from jax.experimental.pallas import tpu as pltpu
from jax.sharding import PartitionSpec as P

MESH = pl.DeviceIdType.MESH
LANES = 128
RUNS = 8
PITCH = 9
LOG2E = 1.4426950408889634
F32 = jnp.float32
BF16 = jnp.bfloat16


def ring_gap(step, size):
    return min(step, size - step)


def time_peers():
    offsets = [(z, y, c) for z in range(4) for y in range(2) for c in range(2)][1:]
    return sorted(offsets, key=lambda o: -(4 * ring_gap(o[0], 4) + 4 * o[1] + o[2]))


def chan_peers():
    offsets = [(y, x) for y in range(2) for x in range(4)][1:]
    return sorted(offsets, key=lambda o: -(2 * o[0] + ring_gap(o[1], 4)))


def scan_runs(weight, value, down):
    run = lax.broadcasted_iota(jnp.int32, weight.shape, 0)
    run = run if down else RUNS - 1 - run
    for gap in (1, 2, 4):
        shift = gap if down else RUNS - gap
        value = value + weight * jnp.where(run >= gap, pltpu.roll(value, shift, 0), 0.0)
        weight = weight * jnp.where(run >= gap, pltpu.roll(weight, shift, 0), 1.0)
    end = slice(RUNS - 1, RUNS) if down else slice(0, 1)
    shift = 1 if down else RUNS - 1
    weight_in = jnp.where(run >= 1, pltpu.roll(weight, shift, 0), 1.0)
    value_in = jnp.where(run >= 1, pltpu.roll(value, shift, 0), 0.0)
    return weight_in, value_in, weight[end], value[end]


def states_kernel(
    sizes,
    fade_hbm,
    update_hbm,
    gain_hbm,
    states,
    power_ref,
    gain,
    fade,
    update,
    keeps,
    pushes,
    own,
    through,
    near,
    runs,
    message,
    inbox,
    powers,
    load_sem,
    gain_sem,
    sent_sem,
    inbox_sem,
    power_sent_sem,
    power_sem,
):
    n_time, n_chan = sizes
    groups, rows, _ = fade.shape
    length = rows * n_time
    half = rows // 2
    steps = half // RUNS
    me_t, me_c = lax.axis_index("time"), lax.axis_index("chan")

    loads = []
    for g in range(groups):
        at = pl.ds(g * LANES, LANES)
        loads.append(
            (
                pltpu.make_async_copy(fade_hbm.at[0, :, at], fade.at[g], load_sem.at[0, g]),
                pltpu.make_async_copy(update_hbm.at[0, :, at], update.at[g], load_sem.at[1, g]),
            )
        )
        for load in loads[g]:
            load.start()
    gain_load = pltpu.make_async_copy(gain_hbm, gain, gain_sem)
    gain_load.start()

    z, y, core = me_t // 4, (me_t // 2) % 2, me_t % 2
    other_times = [
        ((z + dz) % 4) * 4 + ((y + dy) % 2) * 2 + (core + dc) % 2 for dz, dy, dc in time_peers()
    ]
    cy, cx = me_c // 4, me_c % 4
    other_chans = [((cy + dy) % 2) * 4 + (cx + dx) % 4 for dy, dx in chan_peers()]

    barrier = pltpu.get_barrier_semaphore()
    for peer in other_chans:
        pl.semaphore_signal(barrier, inc=1, device_id=(me_t, peer), device_id_type=MESH)
    for peer in other_times:
        pl.semaphore_signal(barrier, inc=1, device_id=(peer, me_c), device_id_type=MESH)

    for g in range(groups):
        for load in loads[g]:
            load.wait()
        ends = []
        summed = None
        for h in range(2):
            slab = 2 * g + h
            for i in range(0, half, 16):
                at = pl.ds(h * half + i, 16)
                rate = fade[g, at]
                keep = jnp.exp2(rate * (-LOG2E / length))
                push = update[g, at].astype(F32)
                for q in range(2):
                    run, step = divmod(i + 8 * q, steps)
                    to = pl.ds(step * PITCH + run, 8, stride=PITCH)
                    keeps[slab, to] = keep[8 * q : 8 * q + 8]
                    pushes[slab, to] = push[8 * q : 8 * q + 8]
                    part = rate[8 * q : 8 * q + 8]
                    summed = part if summed is None else summed + part
            weight = keeps[slab, pl.ds(0, RUNS)]
            ahead = behind = pushes[slab, pl.ds(0, RUNS)]
            for step in range(1, steps):
                keep = keeps[slab, pl.ds(step * PITCH, RUNS)]
                push = pushes[slab, pl.ds(step * PITCH, RUNS)]
                ahead = keep * ahead + push
                behind = behind + weight * push
                weight = weight * keep
            runs[slab, 0] = weight
            runs[slab, 1] = ahead
            runs[slab, 2] = behind
            for gap in (1, 2, 4):
                weight_next, ahead_next, behind_next = (
                    pltpu.roll(x, RUNS - gap, 0) for x in (weight, ahead, behind)
                )
                behind = behind + weight * behind_next
                ahead = ahead_next + weight_next * ahead
                weight = weight * weight_next
            ends.append((weight[:1], ahead[:1], behind[:1]))
        (weight_0, ahead_0, behind_0), (weight_1, ahead_1, behind_1) = ends
        whole = jnp.exp2(jnp.sum(summed, axis=0, keepdims=True) * (-LOG2E / length))
        message[0, 0, g : g + 1] = whole
        message[1, 0, g : g + 1] = whole
        message[0, 1, g : g + 1] = ahead_1 + weight_1 * ahead_0
        message[1, 1, g : g + 1] = behind_0 + weight_0 * behind_1

    pl.semaphore_wait(barrier, len(other_times) + len(other_chans))
    for peer in other_times:
        pltpu.make_async_remote_copy(
            src_ref=message.at[jnp.where(peer > me_t, 0, 1)],
            dst_ref=inbox.at[me_t],
            send_sem=sent_sem,
            recv_sem=inbox_sem.at[me_t],
            device_id=(peer, me_c),
            device_id_type=MESH,
        ).start()

    @pl.loop(0, groups)
    def _(g):
        slabs = (2 * g, 2 * g + 1)
        weights, aheads, behinds = ([runs[slab, k] for slab in slabs] for k in range(3))
        down_0, ahead_0, down_all, ahead_all = scan_runs(weights[0], aheads[0], True)
        down_1, ahead_1, _, _ = scan_runs(weights[1], aheads[1], True)
        up_1, behind_1, up_all, behind_all = scan_runs(weights[1], behinds[1], False)
        up_0, behind_0, _, _ = scan_runs(weights[0], behinds[0], False)
        ahead = [ahead_0, ahead_1 + down_1 * ahead_all]
        down = [down_0, down_1 * down_all]
        behind = [behind_0 + up_0 * behind_all, behind_1]
        up = [up_0 * up_all, up_1]
        for step in range(steps):
            at = pl.ds(step * PITCH, RUNS)
            for h, slab in enumerate(slabs):
                keep = keeps[slab, at]
                ahead[h] = keep * ahead[h] + pushes[slab, at]
                down[h] = keep * down[h]
                own[slab, at] = ahead[h]
                through[slab, at] = down[h]
        for step in range(steps - 1, -1, -1):
            at = pl.ds(step * PITCH, RUNS)
            for h, slab in enumerate(slabs):
                keep = keeps[slab, at]
                behind[h] = keep * behind[h] + pushes[slab, at]
                up[h] = keep * up[h]
                own[slab, at] = own[slab, at] + behind[h]
                near[slab, at] = up[h]

    def taken(k, state):
        pltpu.make_async_copy(inbox.at[k], inbox.at[k], inbox_sem.at[k]).wait()
        return state * inbox[k, 0] + inbox[k, 1]

    zero = jnp.zeros((groups, LANES), F32)
    earlier = lax.fori_loop(0, me_t, taken, zero)
    for g in range(groups):
        entering = jnp.broadcast_to(earlier[g : g + 1], (RUNS, LANES))
        for slab in (2 * g, 2 * g + 1):
            for step in range(steps):
                at = pl.ds(step * PITCH, RUNS)
                own[slab, at] = own[slab, at] + through[slab, at] * entering

    later = lax.fori_loop(0, n_time - 1 - me_t, lambda i, state: taken(n_time - 1 - i, state), zero)

    entering = [jnp.broadcast_to(later[g : g + 1], (RUNS, LANES)) for g in range(groups)]
    for b in range(rows // LANES):
        squares = []
        for row in range(b * LANES, (b + 1) * LANES, 8):
            h, place = divmod(row, half)
            run, step = divmod(place, steps)
            at = pl.ds(step * PITCH + run, 8, stride=PITCH)
            total = None
            for g in range(groups):
                state = own[2 * g + h, at] + near[2 * g + h, at] * entering[g]
                states[g, pl.ds(row, 8)] = state
                square = state * state
                total = square if total is None else total + square
            squares.append(total)
        powers[me_c, b : b + 1] = jnp.sum(jnp.concatenate(squares, axis=0).T, axis=0, keepdims=True)

    for peer in other_chans:
        pltpu.make_async_remote_copy(
            src_ref=powers.at[me_c],
            dst_ref=powers.at[me_c],
            send_sem=power_sent_sem,
            recv_sem=power_sem,
            device_id=(me_t, peer),
            device_id_type=MESH,
        ).start()
    others = powers.at[pl.ds(0, n_chan - 1)]
    pltpu.make_async_copy(others, others, power_sem).wait()
    power = powers[0]
    for k in range(1, n_chan):
        power = power + powers[k]
    power_ref[...] = power

    gain_load.wait()
    others = inbox.at[pl.ds(0, n_time - 1)]
    pltpu.make_async_copy(others, others, sent_sem).wait()
    others = powers.at[pl.ds(0, n_chan - 1)]
    pltpu.make_async_copy(others, others, power_sent_sem).wait()


def norm_kernel(sizes, states, power, gain, out_hbm, out, out_sem):
    channels, length = sizes
    groups, rows, _ = states.shape
    scale = lax.rsqrt(power[...] * (1.0 / channels) + 1e-06 * length)
    stores = []
    for b in range(rows // LANES):
        block = pl.ds(b * LANES, LANES)
        by_row = jnp.broadcast_to(scale[b : b + 1], (LANES, LANES)).T
        for g in range(groups):
            at = pl.ds(g * LANES, LANES)
            out[block, at] = (states[g, block] * by_row * gain[:, at]).astype(BF16)
        stores.append(pltpu.make_async_copy(out.at[block], out_hbm.at[0, block], out_sem.at[b]))
        stores[b].start()
    for store in stores:
        store.wait()


def per_device(fade_rate, update_in, norm_gain):
    n_time, n_chan = lax.axis_size("time"), lax.axis_size("chan")
    _, rows, columns = fade_rate.shape
    groups = columns // LANES
    anywhere = pl.BlockSpec(memory_space=pl.ANY)
    vmem = pl.BlockSpec(memory_space=pltpu.VMEM)
    slabs = pltpu.VMEM((2 * groups, rows // (2 * RUNS) * PITCH, LANES), F32)
    states, power, gain = pl.pallas_call(
        functools.partial(states_kernel, (n_time, n_chan)),
        out_shape=(
            pltpu.VMEM((groups, rows, LANES), F32),
            pltpu.VMEM((rows // LANES, LANES), F32),
            pltpu.VMEM((1, columns), F32),
        ),
        in_specs=[anywhere, anywhere, anywhere],
        out_specs=(vmem, vmem, vmem),
        scratch_shapes=[
            pltpu.VMEM((groups, rows, LANES), F32),
            pltpu.VMEM((groups, rows, LANES), BF16),
            slabs,
            slabs,
            slabs,
            slabs,
            slabs,
            pltpu.VMEM((2 * groups, 3, RUNS, LANES), F32),
            pltpu.VMEM((2, 2, groups, LANES), F32),
            pltpu.VMEM((n_time, 2, groups, LANES), F32),
            pltpu.VMEM((n_chan, rows // LANES, LANES), F32),
            pltpu.SemaphoreType.DMA((2, groups)),
            pltpu.SemaphoreType.DMA,
            pltpu.SemaphoreType.DMA,
            pltpu.SemaphoreType.DMA((n_time,)),
            pltpu.SemaphoreType.DMA,
            pltpu.SemaphoreType.DMA,
        ],
        compiler_params=pltpu.CompilerParams(collective_id=0, has_side_effects=True),
        name="filter_states",
    )(fade_rate, update_in, norm_gain.reshape(1, columns))
    states, power, gain = (
        pltpu.with_memory_space_constraint(x, pltpu.VMEM) for x in (states, power, gain)
    )
    return pl.pallas_call(
        functools.partial(norm_kernel, (columns * n_chan, rows * n_time)),
        out_shape=jax.ShapeDtypeStruct((1, rows, columns), BF16),
        in_specs=[vmem, vmem, vmem],
        out_specs=anywhere,
        scratch_shapes=[
            pltpu.VMEM((rows, columns), BF16),
            pltpu.SemaphoreType.DMA((rows // LANES,)),
        ],
        name="channel_norm",
    )(states, power, gain)


def solution(mesh):
    return jax.shard_map(
        per_device,
        mesh=mesh,
        in_specs=(P(None, "time", "chan"), P(None, "time", "chan"), P("chan")),
        out_specs=P(None, "time", "chan"),
        check_vma=False,
    )
```

time: 18 us -> 17.4 us (0.967)
  local copies, waits for them, and re-layouts: 0.8 us -> 0 us
  Pallas kernels: 17 us -> 17.2 us
    unnamed x1 -> x0, local copies, waits for them, and re-layouts: 0.8 us -> none
    pallas_call x1 -> x2, Pallas kernels: 17 us -> 17.2 us  [the longest x1 16.3 us: per_device(): pl.pallas_call(functools.partial(states_kernel, (n_time, n_chan)), out_sh...]
where the time goes in v3:
time: 17.4 us; the launch traced here: 17.2 us
  Pallas kernels  17.2 us (99%)
    pallas_call x1, Pallas kernels, per_device(): pl.pallas_call(functools.partial(states_kernel, (n_time, n_chan)), out_sh...  16.3 us
    pallas_call x1, Pallas kernels, per_device(): pl.pallas_call(functools.partial(norm_kernel, (columns * n_chan, rows * n...  0.95 us

profile of v3, /device:TPU:0, one launch (start us, length us, event | category | flops | bytes accessed | tf_op | source)
XLA Modules:
  0.0 17.2 jit_solution(16223052708470382303)
XLA Ops:
  0.0 16.3 %filter_states.1 = (f32[4,512,128]{2,1,0:T(8,128)S(1)}, f32[4,128]{1,0:T(4,128)S(1)}, f32[1,512]{1,0:T(1,128)S(1)}) custom-call(f32[1,512,512]{2,1,0:T(8,128)} %fade_hbm.1, bf16[1,512,512]{2,1,0:T(8,128)(2,1)} %update_hbm.1, f32[1,512]{1,0:T(1,128)} %bitcast.1), custom_call_target="tpu_custom_call" | custom-call | tf_op jit(solution)/shard_map/filter_states/pallas_call | solution.py:270
  16.3 0.9 %channel_norm.1 = bf16[1,512,512]{2,1,0:T(8,128)(2,1)} custom-call(f32[4,512,128]{2,1,0:T(8,128)S(1)} %get-tuple-element.8.states, f32[4,128]{1,0:T(4,128)S(1)} %get-tuple-element.9.power, f32[1,512]{1,0:T(1,128)S(1)} %get-tuple-element.10.gain), custom_call_target="tpu_custom_call" | custom-call | tf_op jit(solution)/shard_map/channel_norm/pallas_call | solution.py:304

commit v4 on v3

--- a/solution.py
+++ b/solution.py
@@ -42,6 +42,10 @@
     weight_in = jnp.where(run >= 1, pltpu.roll(weight, shift, 0), 1.0)
     value_in = jnp.where(run >= 1, pltpu.roll(value, shift, 0), 0.0)
     return weight_in, value_in, weight[end], value[end]
+
+
+def arrived(like, sem):
+    pltpu.make_async_copy(like, like, sem).wait()
 
 
 def states_kernel(
@@ -67,8 +71,9 @@
     gain_sem,
     sent_sem,
     inbox_sem,
-    power_sent_sem,
     power_sem,
+    near_sem,
+    far_sem,
 ):
     n_time, n_chan = sizes
     groups, rows, _ = fade.shape
@@ -77,17 +82,10 @@
     steps = half // RUNS
     me_t, me_c = lax.axis_index("time"), lax.axis_index("chan")
 
-    loads = []
     for g in range(groups):
         at = pl.ds(g * LANES, LANES)
-        loads.append(
-            (
-                pltpu.make_async_copy(fade_hbm.at[0, :, at], fade.at[g], load_sem.at[0, g]),
-                pltpu.make_async_copy(update_hbm.at[0, :, at], update.at[g], load_sem.at[1, g]),
-            )
-        )
-        for load in loads[g]:
-            load.start()
+        pltpu.make_async_copy(fade_hbm.at[0, :, at], fade.at[g], load_sem.at[g]).start()
+        pltpu.make_async_copy(update_hbm.at[0, :, at], update.at[g], load_sem.at[g]).start()
     gain_load = pltpu.make_async_copy(gain_hbm, gain, gain_sem)
     gain_load.start()
 
@@ -98,15 +96,16 @@
     cy, cx = me_c // 4, me_c % 4
     other_chans = [((cy + dy) % 2) * 4 + (cx + dx) % 4 for dy, dx in chan_peers()]
 
+    neighbours = [cy * 4 + (cx + 1) % 4, cy * 4 + (cx + 3) % 4, (1 - cy) * 4 + cx]
+
     barrier = pltpu.get_barrier_semaphore()
-    for peer in other_chans:
+    for peer in neighbours:
         pl.semaphore_signal(barrier, inc=1, device_id=(me_t, peer), device_id_type=MESH)
     for peer in other_times:
         pl.semaphore_signal(barrier, inc=1, device_id=(peer, me_c), device_id_type=MESH)
 
     for g in range(groups):
-        for load in loads[g]:
-            load.wait()
+        arrived(fade.at[pl.ds(0, 3), pl.ds(0, half)], load_sem.at[g])
         ends = []
         summed = None
         for h in range(2):
@@ -149,16 +148,19 @@
         message[0, 1, g : g + 1] = ahead_1 + weight_1 * ahead_0
         message[1, 1, g : g + 1] = behind_0 + weight_0 * behind_1
 
-    pl.semaphore_wait(barrier, len(other_times) + len(other_chans))
+    pl.semaphore_wait(barrier, len(other_times) + len(neighbours))
     for peer in other_times:
         pltpu.make_async_remote_copy(
             src_ref=message.at[jnp.where(peer > me_t, 0, 1)],
             dst_ref=inbox.at[me_t],
             send_sem=sent_sem,
-            recv_sem=inbox_sem.at[me_t],
+            recv_sem=inbox_sem.at[jnp.where(peer > me_t, 0, 1)],
             device_id=(peer, me_c),
             device_id_type=MESH,
         ).start()
+
+    for peer in neighbours:
+        pl.semaphore_signal(near_sem, inc=1, device_id=(me_t, peer), device_id_type=MESH)
 
     @pl.loop(0, groups)
     def _(g):
@@ -189,9 +191,18 @@
                 own[slab, at] = own[slab, at] + behind[h]
                 near[slab, at] = up[h]
 
+    pl.semaphore_wait(near_sem, len(neighbours))
+    for peer in neighbours:
+        pl.semaphore_signal(far_sem, inc=1, device_id=(me_t, peer), device_id_type=MESH)
+
     def taken(k, state):
-        pltpu.make_async_copy(inbox.at[k], inbox.at[k], inbox_sem.at[k]).wait()
         return state * inbox[k, 0] + inbox[k, 1]
+
+    for k in range(1, n_time):
+
+        @pl.when(me_t == k)
+        def _():
+            arrived(inbox.at[pl.ds(0, k)], inbox_sem.at[0])
 
     zero = jnp.zeros((groups, LANES), F32)
     earlier = lax.fori_loop(0, me_t, taken, zero)
@@ -201,6 +212,12 @@
             for step in range(steps):
                 at = pl.ds(step * PITCH, RUNS)
                 own[slab, at] = own[slab, at] + through[slab, at] * entering
+
+    for k in range(1, n_time):
+
+        @pl.when(me_t == n_time - 1 - k)
+        def _():
+            arrived(inbox.at[pl.ds(0, k)], inbox_sem.at[1])
 
     later = lax.fori_loop(0, n_time - 1 - me_t, lambda i, state: taken(n_time - 1 - i, state), zero)
 
@@ -220,27 +237,25 @@
             squares.append(total)
         powers[me_c, b : b + 1] = jnp.sum(jnp.concatenate(squares, axis=0).T, axis=0, keepdims=True)
 
+    pl.semaphore_wait(far_sem, len(neighbours))
     for peer in other_chans:
         pltpu.make_async_remote_copy(
             src_ref=powers.at[me_c],
             dst_ref=powers.at[me_c],
-            send_sem=power_sent_sem,
+            send_sem=sent_sem,
             recv_sem=power_sem,
             device_id=(me_t, peer),
             device_id_type=MESH,
         ).start()
-    others = powers.at[pl.ds(0, n_chan - 1)]
-    pltpu.make_async_copy(others, others, power_sem).wait()
+    arrived(powers.at[pl.ds(0, n_chan - 1)], power_sem)
     power = powers[0]
     for k in range(1, n_chan):
         power = power + powers[k]
     power_ref[...] = power
 
     gain_load.wait()
-    others = inbox.at[pl.ds(0, n_time - 1)]
-    pltpu.make_async_copy(others, others, sent_sem).wait()
-    others = powers.at[pl.ds(0, n_chan - 1)]
-    pltpu.make_async_copy(others, others, power_sent_sem).wait()
+    sent = 2 * groups * (n_time - 1) + rows // LANES * (n_chan - 1)
+    arrived(fade.at[0, pl.ds(0, sent)], sent_sem)
 
 
 def norm_kernel(sizes, states, power, gain, out_hbm, out, out_sem):
@@ -288,12 +303,13 @@
             pltpu.VMEM((2, 2, groups, LANES), F32),
             pltpu.VMEM((n_time, 2, groups, LANES), F32),
             pltpu.VMEM((n_chan, rows // LANES, LANES), F32),
-            pltpu.SemaphoreType.DMA((2, groups)),
+            pltpu.SemaphoreType.DMA((groups,)),
             pltpu.SemaphoreType.DMA,
             pltpu.SemaphoreType.DMA,
-            pltpu.SemaphoreType.DMA((n_time,)),
+            pltpu.SemaphoreType.DMA((2,)),
             pltpu.SemaphoreType.DMA,
-            pltpu.SemaphoreType.DMA,
+            pltpu.SemaphoreType.REGULAR,
+            pltpu.SemaphoreType.REGULAR,
         ],
         compiler_params=pltpu.CompilerParams(collective_id=0, has_side_effects=True),
         name="filter_states",

time: 17.4 us -> 16.9 us (0.971)
  Pallas kernels: 17.2 us -> 16.8 us
    pallas_call x1, Pallas kernels: 16.3 us -> 15.9 us  [per_device(): pl.pallas_call(functools.partial(states_kernel, (n_time, n_chan)), out_sh...]
where the time goes in v4:
time: 16.9 us; the launch traced here: 16.8 us
  Pallas kernels  16.8 us (99%)
    pallas_call x1, Pallas kernels, per_device(): pl.pallas_call(functools.partial(states_kernel, (n_time, n_chan)), out_sh...  15.9 us
    pallas_call x1, Pallas kernels, per_device(): pl.pallas_call(functools.partial(norm_kernel, (columns * n_chan, rows * n...  0.95 us

profile of v4, /device:TPU:0, one launch (start us, length us, event | category | flops | bytes accessed | tf_op | source)
XLA Modules:
  0.0 16.8 jit_solution(9544176597736389690)
XLA Ops:
  0.0 15.9 %filter_states.1 = (f32[4,512,128]{2,1,0:T(8,128)S(1)}, f32[4,128]{1,0:T(4,128)S(1)}, f32[1,512]{1,0:T(1,128)S(1)}) custom-call(f32[1,512,512]{2,1,0:T(8,128)} %fade_hbm.1, bf16[1,512,512]{2,1,0:T(8,128)(2,1)} %update_hbm.1, f32[1,512]{1,0:T(1,128)} %bitcast.1), custom_call_target="tpu_custom_call" | custom-call | tf_op jit(solution)/shard_map/filter_states/pallas_call | solution.py:285
  15.9 0.9 %channel_norm.1 = bf16[1,512,512]{2,1,0:T(8,128)(2,1)} custom-call(f32[4,512,128]{2,1,0:T(8,128)S(1)} %get-tuple-element.8.states, f32[4,128]{1,0:T(4,128)S(1)} %get-tuple-element.9.power, f32[1,512]{1,0:T(1,128)S(1)} %get-tuple-element.10.gain), custom_call_target="tpu_custom_call" | custom-call | tf_op jit(solution)/shard_map/channel_norm/pallas_call | solution.py:320

commit v5 on v4

v5 whole, which is shorter than its diff:
```python
import functools

import jax
import jax.numpy as jnp
from jax import lax
from jax.experimental import pallas as pl
from jax.experimental.pallas import tpu as pltpu
from jax.sharding import PartitionSpec as P

MESH = pl.DeviceIdType.MESH
LANES = 128
RUNS = 8
PIECES = 4
PLANE = 4
CHAN_RING = 4
PITCH = 17
LOG2E = 1.4426950408889634
F32 = jnp.float32
BF16 = jnp.bfloat16


def scan_runs(weight, value, down):
    run = lax.broadcasted_iota(jnp.int32, weight.shape, 0)
    run = run if down else RUNS - 1 - run
    for gap in (1, 2, 4):
        shift = gap if down else RUNS - gap
        value = value + weight * jnp.where(run >= gap, pltpu.roll(value, shift, 0), 0.0)
        weight = weight * jnp.where(run >= gap, pltpu.roll(weight, shift, 0), 1.0)
    shift = 1 if down else RUNS - 1
    weight = jnp.where(run >= 1, pltpu.roll(weight, shift, 0), 1.0)
    return weight, jnp.where(run >= 1, pltpu.roll(value, shift, 0), 0.0)


def arrived(like, sem):
    pltpu.make_async_copy(like, like, sem).wait()


def told(sem, times):
    @pl.when(times > 0)
    def _():
        pl.semaphore_wait(sem, times)


def states_kernel(
    sizes,
    fade_hbm,
    update_hbm,
    gain_hbm,
    states,
    power_ref,
    fade,
    update,
    gain,
    flows,
    own,
    through,
    pieces,
    runs,
    message,
    inbox,
    powers,
    load_sem,
    gain_sem,
    sent_sem,
    inbox_sem,
    power_sem,
    come_sem,
    near_sem,
    middle_sem,
    far_sem,
):
    n_time, n_chan = sizes
    groups, rows, _ = fade.shape
    length = rows * n_time
    steps = rows // (RUNS * PIECES)
    for g in range(groups):
        at = pl.ds(g * LANES, LANES)
        pltpu.make_async_copy(fade_hbm.at[0, :, at], fade.at[g], load_sem.at[g]).start()
        pltpu.make_async_copy(update_hbm.at[0, :, at], update.at[g], load_sem.at[g]).start()
    gain_load = pltpu.make_async_copy(gain_hbm, gain, gain_sem)
    gain_load.start()
    pl.delay(1)

    me_t, me_c = lax.axis_index("time"), lax.axis_index("chan")
    row, cx = me_c // CHAN_RING, me_c % CHAN_RING
    around = [
        row * CHAN_RING + (cx + 1) % CHAN_RING,
        row * CHAN_RING + (cx + CHAN_RING - 1) % CHAN_RING,
        me_c + CHAN_RING - 2 * CHAN_RING * row,
    ]
    plane = me_t // PLANE
    lower_around = sum(jnp.where(peer < me_c, 1, 0) for peer in around)

    barrier = pltpu.get_barrier_semaphore()
    for peer in around:

        @pl.when(peer > me_c)
        def _():
            pl.semaphore_signal(barrier, inc=1, device_id=(me_t, peer), device_id_type=MESH)

    @pl.loop(me_t + 1, n_time)
    def _(k):
        pl.semaphore_signal(barrier, inc=1, device_id=(k, me_c), device_id_type=MESH)

    def spread(g):
        summed = None
        for i in range(0, rows, 16):
            at = pl.ds(i, 16)
            rate = fade[g, at]
            keep = jnp.exp2(rate * (-LOG2E / length))
            part = rate[:8] + rate[8:]
            summed = part if summed is None else summed + part
            push = update[g, at].astype(F32)
            for q in range(2):
                run, place = divmod(i + 8 * q, rows // RUNS)
                piece, step = divmod(place, steps)
                to = pl.ds(step * PITCH + run, 8, stride=PITCH)
                to_push = pl.ds(step * PITCH + RUNS + run, 8, stride=PITCH)
                flows[g * PIECES + piece, to] = keep[8 * q : 8 * q + 8]
                flows[g * PIECES + piece, to_push] = push[8 * q : 8 * q + 8]
        whole = jnp.exp2(jnp.sum(summed, axis=0, keepdims=True) * (-LOG2E / length))
        message[0, 0, g : g + 1] = whole
        message[1, 0, g : g + 1] = whole

    def summary(g):
        slabs = range(g * PIECES, (g + 1) * PIECES)
        weights = [flows[slab, pl.ds(0, RUNS)] for slab in slabs]
        aheads = [flows[slab, pl.ds(RUNS, RUNS)] for slab in slabs]
        behinds = list(aheads)
        for step in range(1, steps):
            at, at_push = pl.ds(step * PITCH, RUNS), pl.ds(step * PITCH + RUNS, RUNS)
            for p, slab in enumerate(slabs):
                keep, push = flows[slab, at], flows[slab, at_push]
                aheads[p] = keep * aheads[p] + push
                behinds[p] = behinds[p] + weights[p] * push
                weights[p] = weights[p] * keep
        for p, slab in enumerate(slabs):
            pieces[slab, 0], pieces[slab, 1], pieces[slab, 2] = weights[p], aheads[p], behinds[p]
        parts = list(zip(weights, aheads, behinds))
        while len(parts) > 1:
            parts = [
                (w0 * w1, a1 + w1 * a0, b0 + w0 * b1)
                for (w0, a0, b0), (w1, a1, b1) in zip(parts[::2], parts[1::2])
            ]
        weight, ahead, behind = parts[0]
        runs[g, 0], runs[g, 1], runs[g, 2] = weight, ahead, behind
        for gap in (1, 2, 4):
            weight_next, ahead_next, behind_next = (
                pltpu.roll(x, RUNS - gap, 0) for x in (weight, ahead, behind)
            )
            behind = behind + weight * behind_next
            ahead = ahead_next + weight_next * ahead
            weight = weight * weight_next
        message[0, 1, g : g + 1] = ahead[:1]
        message[1, 1, g : g + 1] = behind[:1]

    for g in range(groups + 1):
        if g < groups:
            arrived(fade.at[pl.ds(0, 3), pl.ds(0, rows // 2)], load_sem.at[g])
            spread(g)
        if g > 0:
            summary(g - 1)

    def send_summary(k, way):
        pltpu.make_async_remote_copy(
            src_ref=message.at[way],
            dst_ref=inbox.at[me_t],
            send_sem=sent_sem,
            recv_sem=inbox_sem.at[way],
            device_id=(k, me_c),
            device_id_type=MESH,
        ).start()

    told(barrier, me_t + lower_around)
    @pl.loop(0, me_t)
    def _(k):
        send_summary(k, 1)

    for peer in around:

        @pl.when(peer < me_c)
        def _():
            pl.semaphore_signal(near_sem, inc=1, device_id=(me_t, peer), device_id_type=MESH)

    @pl.loop(0, me_t)
    def _(k):
        come = come_sem.at[plane]
        pl.semaphore_signal(come, inc=1, device_id=(k, me_c), device_id_type=MESH)

    told(come_sem.at[plane], PLANE - 1 - me_t % PLANE)

    @pl.loop(me_t + 1, (plane + 1) * PLANE)
    def _(k):
        send_summary(k, 0)

    def send_plane(to):
        @pl.when(to > plane)
        def _():
            pl.semaphore_wait(come_sem.at[to], PLANE)
            for k in range(to * PLANE, (to + 1) * PLANE):
                send_summary(k, 0)

    def tell_around(sem):
        for peer in around:
            pl.semaphore_signal(sem, inc=1, device_id=(me_t, peer), device_id_type=MESH)

    @pl.loop(0, groups)
    def _(g):
        slabs = [g * PIECES + p for p in range(PIECES)]
        down_in, ahead_in = scan_runs(runs[g, 0], runs[g, 1], True)
        up_in, behind_in = scan_runs(runs[g, 0], runs[g, 2], False)
        down, ahead, up, behind = [], [], [], []
        for slab in slabs:
            down.append(down_in)
            ahead.append(ahead_in)
            down_in = down_in * pieces[slab, 0]
            ahead_in = ahead_in * pieces[slab, 0] + pieces[slab, 1]
        for slab in slabs[::-1]:
            up.insert(0, up_in)
            behind.insert(0, behind_in)
            up_in = up_in * pieces[slab, 0]
            behind_in = behind_in * pieces[slab, 0] + pieces[slab, 2]
        for step in range(steps):
            at, at_2 = pl.ds(step * PITCH, RUNS), pl.ds(step * PITCH + RUNS, RUNS)
            for p, slab in enumerate(slabs):
                keep = flows[slab, at]
                ahead[p] = keep * ahead[p] + flows[slab, at_2]
                down[p] = keep * down[p]
                own[slab, at] = ahead[p]
                through[slab, at] = down[p]
        for step in range(steps - 1, -1, -1):
            at, at_2 = pl.ds(step * PITCH, RUNS), pl.ds(step * PITCH + RUNS, RUNS)
            for p, slab in enumerate(slabs):
                keep = flows[slab, at]
                behind[p] = keep * behind[p] + flows[slab, at_2]
                up[p] = keep * up[p]
                own[slab, at] = own[slab, at] + behind[p]
                own[slab, at_2] = up[p]

    told(near_sem, len(around) - lower_around)
    tell_around(middle_sem)
    for to in range(1, n_time // PLANE):
        send_plane(to)
    pl.semaphore_wait(middle_sem, len(around))
    tell_around(far_sem)

    def taken(k, state):
        return state * inbox[k, 0] + inbox[k, 1]

    for k in range(1, n_time):

        @pl.when(me_t == k)
        def _():
            arrived(inbox.at[pl.ds(0, k)], inbox_sem.at[0])

    zero = jnp.zeros((groups, LANES), F32)
    earlier = lax.fori_loop(0, me_t, taken, zero)
    for g in range(groups):
        entering = jnp.broadcast_to(earlier[g : g + 1], (RUNS, LANES))
        for slab in range(g * PIECES, (g + 1) * PIECES):
            for step in range(steps):
                at = pl.ds(step * PITCH, RUNS)
                own[slab, at] = own[slab, at] + through[slab, at] * entering

    for k in range(1, n_time):

        @pl.when(me_t == n_time - 1 - k)
        def _():
            arrived(inbox.at[pl.ds(0, k)], inbox_sem.at[1])

    later = lax.fori_loop(0, n_time - 1 - me_t, lambda i, state: taken(n_time - 1 - i, state), zero)

    entering = [jnp.broadcast_to(later[g : g + 1], (RUNS, LANES)) for g in range(groups)]

    def state_tile(g, row):
        run, place = divmod(row, rows // RUNS)
        piece, step = divmod(place, steps)
        slab, start = g * PIECES + piece, step * PITCH + run
        near = own[slab, pl.ds(start + RUNS, 8, stride=PITCH)]
        return own[slab, pl.ds(start, 8, stride=PITCH)] + near * entering[g]

    for b in range(rows // LANES):
        squares = []
        for row in range(b * LANES, (b + 1) * LANES, 8):
            total = None
            for g in range(groups):
                state = state_tile(g, row)
                square = state * state
                total = square if total is None else total + square
            squares.append(total)
        powers[me_c, b : b + 1] = jnp.sum(jnp.concatenate(squares, axis=0).T, axis=0, keepdims=True)

    pl.semaphore_wait(far_sem, len(around))
    for k in range(n_chan - 1):
        pltpu.make_async_remote_copy(
            src_ref=powers.at[me_c],
            dst_ref=powers.at[me_c],
            send_sem=sent_sem,
            recv_sem=power_sem,
            device_id=(me_t, k + jnp.where(k >= me_c, 1, 0)),
            device_id_type=MESH,
        ).start()
    gain_load.wait()
    for g in range(groups):
        gains = jnp.broadcast_to(gain[:, g * LANES : (g + 1) * LANES], (RUNS, LANES))
        for row in range(0, rows, 8):
            states[g, pl.ds(row, 8)] = state_tile(g, row) * gains
    arrived(powers.at[pl.ds(0, n_chan - 1)], power_sem)
    power = powers[0]
    for k in range(1, n_chan):
        power = power + powers[k]
    power_ref[...] = power

    sent = 2 * groups * (n_time - 1) + rows // LANES * (n_chan - 1)
    arrived(fade.at[0, pl.ds(0, sent)], sent_sem)


def norm_kernel(sizes, states, power, out_hbm, out, out_sem):
    channels, length = sizes
    groups, rows, _ = states.shape
    scale = lax.rsqrt(power[...] * (1.0 / channels) + 1e-06 * length)
    stores = []
    for b in range(rows // LANES):
        block = pl.ds(b * LANES, LANES)
        by_row = jnp.broadcast_to(scale[b : b + 1], (LANES, LANES)).T
        for g in range(groups):
            at = pl.ds(g * LANES, LANES)
            out[block, at] = (states[g, block] * by_row).astype(BF16)
        stores.append(pltpu.make_async_copy(out.at[block], out_hbm.at[0, block], out_sem.at[b]))
        stores[b].start()
    for store in stores:
        store.wait()


def per_device(fade_rate, update_in, norm_gain):
    n_time, n_chan = lax.axis_size("time"), lax.axis_size("chan")
    _, rows, columns = fade_rate.shape
    groups = columns // LANES
    anywhere = pl.BlockSpec(memory_space=pl.ANY)
    vmem = pl.BlockSpec(memory_space=pltpu.VMEM)
    slabs = pltpu.VMEM((PIECES * groups, rows // (PIECES * RUNS) * PITCH, LANES), F32)
    states, power = pl.pallas_call(
        functools.partial(states_kernel, (n_time, n_chan)),
        out_shape=(
            pltpu.VMEM((groups, rows, LANES), F32),
            pltpu.VMEM((rows // LANES, LANES), F32),
        ),
        in_specs=[anywhere, anywhere, anywhere],
        out_specs=(vmem, vmem),
        scratch_shapes=[
            pltpu.VMEM((groups, rows, LANES), F32),
            pltpu.VMEM((groups, rows, LANES), BF16),
            pltpu.VMEM((1, columns), F32),
            slabs,
            slabs,
            slabs,
            pltpu.VMEM((PIECES * groups, 3, RUNS, LANES), F32),
            pltpu.VMEM((groups, 3, RUNS, LANES), F32),
            pltpu.VMEM((2, 2, groups, LANES), F32),
            pltpu.VMEM((n_time, 2, groups, LANES), F32),
            pltpu.VMEM((n_chan, rows // LANES, LANES), F32),
            pltpu.SemaphoreType.DMA((groups,)),
            pltpu.SemaphoreType.DMA,
            pltpu.SemaphoreType.DMA,
            pltpu.SemaphoreType.DMA((2,)),
            pltpu.SemaphoreType.DMA,
            pltpu.SemaphoreType.REGULAR((n_time // PLANE,)),
            pltpu.SemaphoreType.REGULAR,
            pltpu.SemaphoreType.REGULAR,
            pltpu.SemaphoreType.REGULAR,
        ],
        compiler_params=pltpu.CompilerParams(collective_id=0, has_side_effects=True),
        name="filter_states",
    )(fade_rate, update_in, norm_gain.reshape(1, columns))
    states, power = (pltpu.with_memory_space_constraint(x, pltpu.VMEM) for x in (states, power))
    return pl.pallas_call(
        functools.partial(norm_kernel, (columns * n_chan, rows * n_time)),
        out_shape=jax.ShapeDtypeStruct((1, rows, columns), BF16),
        in_specs=[vmem, vmem],
        out_specs=anywhere,
        scratch_shapes=[
            pltpu.VMEM((rows, columns), BF16),
            pltpu.SemaphoreType.DMA((rows // LANES,)),
        ],
        name="channel_norm",
    )(states, power)


def solution(mesh):
    return jax.shard_map(
        per_device,
        mesh=mesh,
        in_specs=(P(None, "time", "chan"), P(None, "time", "chan"), P("chan")),
        out_specs=P(None, "time", "chan"),
        check_vma=False,
    )
```

time: 16.9 us -> 16.8 us (level)
  Pallas kernels: 16.8 us -> 16.5 us
    pallas_call x1, Pallas kernels: 15.9 us -> 15.6 us  [per_device(): pl.pallas_call(functools.partial(states_kernel, (n_time, n_chan)), out_sh...]
where the time goes in v5:
time: 16.8 us; the launch traced here: 16.6 us
  Pallas kernels  16.5 us (98%)
    pallas_call x1, Pallas kernels, per_device(): pl.pallas_call(functools.partial(states_kernel, (n_time, n_chan)), out_sh...  15.6 us
    pallas_call x1, Pallas kernels, per_device(): pl.pallas_call(functools.partial(norm_kernel, (columns * n_chan, rows * n...  0.93 us

profile of v5, /device:TPU:0, one launch (start us, length us, event | category | flops | bytes accessed | tf_op | source)
XLA Modules:
  0.0 16.6 jit_solution(5581431523839184647)
XLA Ops:
  0.0 15.6 %filter_states.1 = (f32[4,512,128]{2,1,0:T(8,128)S(1)}, f32[4,128]{1,0:T(4,128)S(1)}) custom-call(f32[1,512,512]{2,1,0:T(8,128)} %fade_hbm.1, bf16[1,512,512]{2,1,0:T(8,128)(2,1)} %update_hbm.1, f32[1,512]{1,0:T(1,128)} %bitcast.1), custom_call_target="tpu_custom_call" | custom-call | tf_op jit(solution)/shard_map/filter_states/pallas_call | solution.py:342
  15.6 0.9 %channel_norm.1 = bf16[1,512,512]{2,1,0:T(8,128)(2,1)} custom-call(f32[4,512,128]{2,1,0:T(8,128)S(1)} %get-tuple-element.7.states, f32[4,128]{1,0:T(4,128)S(1)} %get-tuple-element.8.power), custom_call_target="tpu_custom_call" | custom-call | tf_op jit(solution)/shard_map/channel_norm/pallas_call | solution.py:376

commit v6 on v5

--- a/solution.py
+++ b/solution.py
@@ -122,44 +122,55 @@
         message[0, 0, g : g + 1] = whole
         message[1, 0, g : g + 1] = whole
 
-    def summary(g):
+    def backward_part(g):
         slabs = range(g * PIECES, (g + 1) * PIECES)
         weights = [flows[slab, pl.ds(0, RUNS)] for slab in slabs]
-        aheads = [flows[slab, pl.ds(RUNS, RUNS)] for slab in slabs]
-        behinds = list(aheads)
+        behinds = [flows[slab, pl.ds(RUNS, RUNS)] for slab in slabs]
         for step in range(1, steps):
             at, at_push = pl.ds(step * PITCH, RUNS), pl.ds(step * PITCH + RUNS, RUNS)
             for p, slab in enumerate(slabs):
-                keep, push = flows[slab, at], flows[slab, at_push]
-                aheads[p] = keep * aheads[p] + push
-                behinds[p] = behinds[p] + weights[p] * push
-                weights[p] = weights[p] * keep
+                behinds[p] = behinds[p] + weights[p] * flows[slab, at_push]
+                weights[p] = weights[p] * flows[slab, at]
         for p, slab in enumerate(slabs):
-            pieces[slab, 0], pieces[slab, 1], pieces[slab, 2] = weights[p], aheads[p], behinds[p]
-        parts = list(zip(weights, aheads, behinds))
+            pieces[slab, 0], pieces[slab, 2] = weights[p], behinds[p]
+        parts = list(zip(weights, behinds))
         while len(parts) > 1:
             parts = [
-                (w0 * w1, a1 + w1 * a0, b0 + w0 * b1)
-                for (w0, a0, b0), (w1, a1, b1) in zip(parts[::2], parts[1::2])
+                (w0 * w1, b0 + w0 * b1) for (w0, b0), (w1, b1) in zip(parts[::2], parts[1::2])
             ]
-        weight, ahead, behind = parts[0]
-        runs[g, 0], runs[g, 1], runs[g, 2] = weight, ahead, behind
+        weight, behind = parts[0]
+        runs[g, 0], runs[g, 2] = weight, behind
         for gap in (1, 2, 4):
-            weight_next, ahead_next, behind_next = (
-                pltpu.roll(x, RUNS - gap, 0) for x in (weight, ahead, behind)
-            )
-            behind = behind + weight * behind_next
-            ahead = ahead_next + weight_next * ahead
+            behind = behind + weight * pltpu.roll(behind, RUNS - gap, 0)
+            weight = weight * pltpu.roll(weight, RUNS - gap, 0)
+        message[1, 1, g : g + 1] = behind[:1]
+
+    def forward_part(g):
+        slabs = range(g * PIECES, (g + 1) * PIECES)
+        aheads = [flows[slab, pl.ds(RUNS, RUNS)] for slab in slabs]
+        for step in range(1, steps):
+            at, at_push = pl.ds(step * PITCH, RUNS), pl.ds(step * PITCH + RUNS, RUNS)
+            for p, slab in enumerate(slabs):
+                aheads[p] = flows[slab, at] * aheads[p] + flows[slab, at_push]
+        ahead = aheads[0]
+        pieces[g * PIECES, 1] = ahead
+        for p in range(1, PIECES):
+            pieces[g * PIECES + p, 1] = aheads[p]
+            ahead = aheads[p] + pieces[g * PIECES + p, 0] * ahead
+        weight = runs[g, 0]
+        runs[g, 1] = ahead
+        for gap in (1, 2, 4):
+            weight_next = pltpu.roll(weight, RUNS - gap, 0)
+            ahead = pltpu.roll(ahead, RUNS - gap, 0) + weight_next * ahead
             weight = weight * weight_next
         message[0, 1, g : g + 1] = ahead[:1]
-        message[1, 1, g : g + 1] = behind[:1]
 
     for g in range(groups + 1):
         if g < groups:
             arrived(fade.at[pl.ds(0, 3), pl.ds(0, rows // 2)], load_sem.at[g])
             spread(g)
         if g > 0:
-            summary(g - 1)
+            backward_part(g - 1)
 
     def send_summary(k, way):
         pltpu.make_async_remote_copy(
@@ -186,6 +197,10 @@
     def _(k):
         come = come_sem.at[plane]
         pl.semaphore_signal(come, inc=1, device_id=(k, me_c), device_id_type=MESH)
+
+    for g in range(groups):
+        forward_part(g)
+    inbox[me_t] = message[0]
 
     told(come_sem.at[plane], PLANE - 1 - me_t % PLANE)
 
@@ -268,7 +283,9 @@
         def _():
             arrived(inbox.at[pl.ds(0, k)], inbox_sem.at[1])
 
-    later = lax.fori_loop(0, n_time - 1 - me_t, lambda i, state: taken(n_time - 1 - i, state), zero)
+    later = zero
+    for k in range(n_time - 1, 0, -1):
+        later = jnp.where(k > me_t, taken(k, later), later)
 
     entering = [jnp.broadcast_to(later[g : g + 1], (RUNS, LANES)) for g in range(groups)]
 

time: 16.8 us -> 16.7 us (level)
  no operation moved by 1% of the time
where the time goes in v6:
time: 16.7 us; the launch traced here: 16.5 us
  Pallas kernels  16.5 us (99%)
    pallas_call x1, Pallas kernels, per_device(): pl.pallas_call(functools.partial(states_kernel, (n_time, n_chan)), out_sh...  15.6 us
    pallas_call x1, Pallas kernels, per_device(): pl.pallas_call(functools.partial(norm_kernel, (columns * n_chan, rows * n...  0.93 us

profile of v6, /device:TPU:0, one launch (start us, length us, event | category | flops | bytes accessed | tf_op | source)
XLA Modules:
  0.0 16.5 jit_solution(15433383242681804094)
XLA Ops:
  0.0 15.6 %filter_states.1 = (f32[4,512,128]{2,1,0:T(8,128)S(1)}, f32[4,128]{1,0:T(4,128)S(1)}) custom-call(f32[1,512,512]{2,1,0:T(8,128)} %fade_hbm.1, bf16[1,512,512]{2,1,0:T(8,128)(2,1)} %update_hbm.1, f32[1,512]{1,0:T(1,128)} %bitcast.1), custom_call_target="tpu_custom_call" | custom-call | tf_op jit(solution)/shard_map/filter_states/pallas_call | solution.py:359
  15.6 0.9 %channel_norm.1 = bf16[1,512,512]{2,1,0:T(8,128)(2,1)} custom-call(f32[4,512,128]{2,1,0:T(8,128)S(1)} %get-tuple-element.7.states, f32[4,128]{1,0:T(4,128)S(1)} %get-tuple-element.8.power), custom_call_target="tpu_custom_call" | custom-call | tf_op jit(solution)/shard_map/channel_norm/pallas_call | solution.py:393

commit v7 on v6

--- a/solution.py
+++ b/solution.py
@@ -104,7 +104,7 @@
 
     def spread(g):
         summed = None
-        for i in range(0, rows, 16):
+        for i in [run * (rows // RUNS) + p for p in range(0, rows // RUNS, 16) for run in range(RUNS)]:
             at = pl.ds(i, 16)
             rate = fade[g, at]
             keep = jnp.exp2(rate * (-LOG2E / length))
@@ -283,9 +283,16 @@
         def _():
             arrived(inbox.at[pl.ds(0, k)], inbox_sem.at[1])
 
-    later = zero
-    for k in range(n_time - 1, 0, -1):
-        later = jnp.where(k > me_t, taken(k, later), later)
+    joined = [
+        (jnp.where(k > me_t, inbox[k, 0], 1.0), jnp.where(k > me_t, inbox[k, 1], 0.0))
+        for k in range(n_time - 1, 0, -1)
+    ]
+    while len(joined) > 1:
+        joined = [
+            (joined[k][0] * joined[k + 1][0], joined[k][1] * joined[k + 1][0] + joined[k + 1][1])
+            for k in range(0, len(joined) - 1, 2)
+        ] + joined[len(joined) // 2 * 2 :]
+    later = joined[0][1]
 
     entering = [jnp.broadcast_to(later[g : g + 1], (RUNS, LANES)) for g in range(groups)]
 

time: 16.7 us -> 16.7 us (level)
  no operation moved by 1% of the time
where the time goes in v7:
time: 16.7 us; the launch traced here: 16.5 us
  Pallas kernels  16.5 us (99%)
    pallas_call x1, Pallas kernels, per_device(): pl.pallas_call(functools.partial(states_kernel, (n_time, n_chan)), out_sh...  15.5 us
    pallas_call x1, Pallas kernels, per_device(): pl.pallas_call(functools.partial(norm_kernel, (columns * n_chan, rows * n...  0.93 us

profile of v7, /device:TPU:0, one launch (start us, length us, event | category | flops | bytes accessed | tf_op | source)
XLA Modules:
  0.0 16.5 jit_solution(3336571553797045752)
XLA Ops:
  0.0 15.5 %filter_states.1 = (f32[4,512,128]{2,1,0:T(8,128)S(1)}, f32[4,128]{1,0:T(4,128)S(1)}) custom-call(f32[1,512,512]{2,1,0:T(8,128)} %fade_hbm.1, bf16[1,512,512]{2,1,0:T(8,128)(2,1)} %update_hbm.1, f32[1,512]{1,0:T(1,128)} %bitcast.1), custom_call_target="tpu_custom_call" | custom-call | tf_op jit(solution)/shard_map/filter_states/pallas_call | solution.py:366
  15.5 0.9 %channel_norm.1 = bf16[1,512,512]{2,1,0:T(8,128)(2,1)} custom-call(f32[4,512,128]{2,1,0:T(8,128)S(1)} %get-tuple-element.7.states, f32[4,128]{1,0:T(4,128)S(1)} %get-tuple-element.8.power), custom_call_target="tpu_custom_call" | custom-call | tf_op jit(solution)/shard_map/channel_norm/pallas_call | solution.py:400

commit v8 on v7

--- a/solution.py
+++ b/solution.py
@@ -59,8 +59,6 @@
     message,
     inbox,
     powers,
-    load_sem,
-    gain_sem,
     sent_sem,
     inbox_sem,
     power_sem,
@@ -73,34 +71,19 @@
     groups, rows, _ = fade.shape
     length = rows * n_time
     steps = rows // (RUNS * PIECES)
-    for g in range(groups):
-        at = pl.ds(g * LANES, LANES)
-        pltpu.make_async_copy(fade_hbm.at[0, :, at], fade.at[g], load_sem.at[g]).start()
-        pltpu.make_async_copy(update_hbm.at[0, :, at], update.at[g], load_sem.at[g]).start()
-    gain_load = pltpu.make_async_copy(gain_hbm, gain, gain_sem)
-    gain_load.start()
-    pl.delay(1)
-
-    me_t, me_c = lax.axis_index("time"), lax.axis_index("chan")
-    row, cx = me_c // CHAN_RING, me_c % CHAN_RING
-    around = [
-        row * CHAN_RING + (cx + 1) % CHAN_RING,
-        row * CHAN_RING + (cx + CHAN_RING - 1) % CHAN_RING,
-        me_c + CHAN_RING - 2 * CHAN_RING * row,
-    ]
-    plane = me_t // PLANE
-    lower_around = sum(jnp.where(peer < me_c, 1, 0) for peer in around)
+    def places():
+        me_t, me_c = lax.axis_index("time"), lax.axis_index("chan")
+        row, cx = me_c // CHAN_RING, me_c % CHAN_RING
+        around = [
+            row * CHAN_RING + (cx + 1) % CHAN_RING,
+            row * CHAN_RING + (cx + CHAN_RING - 1) % CHAN_RING,
+            me_c + CHAN_RING - 2 * CHAN_RING * row,
+        ]
+        plane = me_t // PLANE
+        lower_around = sum(jnp.where(peer < me_c, 1, 0) for peer in around)
+        return me_t, me_c, plane, around, lower_around
 
     barrier = pltpu.get_barrier_semaphore()
-    for peer in around:
-
-        @pl.when(peer > me_c)
-        def _():
-            pl.semaphore_signal(barrier, inc=1, device_id=(me_t, peer), device_id_type=MESH)
-
-    @pl.loop(me_t + 1, n_time)
-    def _(k):
-        pl.semaphore_signal(barrier, inc=1, device_id=(k, me_c), device_id_type=MESH)
 
     def spread(g):
         summed = None
@@ -165,14 +148,7 @@
             weight = weight * weight_next
         message[0, 1, g : g + 1] = ahead[:1]
 
-    for g in range(groups + 1):
-        if g < groups:
-            arrived(fade.at[pl.ds(0, 3), pl.ds(0, rows // 2)], load_sem.at[g])
-            spread(g)
-        if g > 0:
-            backward_part(g - 1)
-
-    def send_summary(k, way):
+    def send_summary(me_t, me_c, k, way):
         pltpu.make_async_remote_copy(
             src_ref=message.at[way],
             dst_ref=inbox.at[me_t],
@@ -182,21 +158,55 @@
             device_id_type=MESH,
         ).start()
 
-    told(barrier, me_t + lower_around)
-    @pl.loop(0, me_t)
-    def _(k):
-        send_summary(k, 1)
-
-    for peer in around:
-
-        @pl.when(peer < me_c)
-        def _():
-            pl.semaphore_signal(near_sem, inc=1, device_id=(me_t, peer), device_id_type=MESH)
-
-    @pl.loop(0, me_t)
-    def _(k):
-        come = come_sem.at[plane]
-        pl.semaphore_signal(come, inc=1, device_id=(k, me_c), device_id_type=MESH)
+    def load_and_send(load_sem, gain_sem):
+        for g in range(groups):
+            at = pl.ds(g * LANES, LANES)
+            pltpu.make_async_copy(fade_hbm.at[0, :, at], fade.at[g], load_sem.at[g]).start()
+            pltpu.make_async_copy(update_hbm.at[0, :, at], update.at[g], load_sem.at[g]).start()
+        gain_load = pltpu.make_async_copy(gain_hbm, gain, gain_sem)
+        gain_load.start()
+        pl.delay(1)
+        me_t, me_c, plane, around, lower_around = places()
+
+        for peer in around:
+
+            @pl.when(peer > me_c)
+            def _():
+                pl.semaphore_signal(barrier, inc=1, device_id=(me_t, peer), device_id_type=MESH)
+
+        @pl.loop(me_t + 1, n_time)
+        def _(k):
+            pl.semaphore_signal(barrier, inc=1, device_id=(k, me_c), device_id_type=MESH)
+
+        for g in range(groups + 1):
+            if g < groups:
+                arrived(fade.at[pl.ds(0, 3), pl.ds(0, rows // 2)], load_sem.at[g])
+                spread(g)
+            if g > 0:
+                backward_part(g - 1)
+
+        told(barrier, me_t + lower_around)
+
+        @pl.loop(0, me_t)
+        def _(k):
+            send_summary(me_t, me_c, k, 1)
+
+        for peer in around:
+
+            @pl.when(peer < me_c)
+            def _():
+                pl.semaphore_signal(near_sem, inc=1, device_id=(me_t, peer), device_id_type=MESH)
+
+        @pl.loop(0, me_t)
+        def _(k):
+            come = come_sem.at[plane]
+            pl.semaphore_signal(come, inc=1, device_id=(k, me_c), device_id_type=MESH)
+
+        gain_load.wait()
+
+    pl.run_scoped(load_and_send, pltpu.SemaphoreType.DMA((groups,)), pltpu.SemaphoreType.DMA)
+
+    me_t, me_c, plane, around, lower_around = places()
 
     for g in range(groups):
         forward_part(g)
@@ -206,14 +216,14 @@
 
     @pl.loop(me_t + 1, (plane + 1) * PLANE)
     def _(k):
-        send_summary(k, 0)
+        send_summary(me_t, me_c, k, 0)
 
     def send_plane(to):
         @pl.when(to > plane)
         def _():
             pl.semaphore_wait(come_sem.at[to], PLANE)
             for k in range(to * PLANE, (to + 1) * PLANE):
-                send_summary(k, 0)
+                send_summary(me_t, me_c, k, 0)
 
     def tell_around(sem):
         for peer in around:
@@ -324,7 +334,6 @@
             device_id=(me_t, k + jnp.where(k >= me_c, 1, 0)),
             device_id_type=MESH,
         ).start()
-    gain_load.wait()
     for g in range(groups):
         gains = jnp.broadcast_to(gain[:, g * LANES : (g + 1) * LANES], (RUNS, LANES))
         for row in range(0, rows, 8):
@@ -343,17 +352,14 @@
     channels, length = sizes
     groups, rows, _ = states.shape
     scale = lax.rsqrt(power[...] * (1.0 / channels) + 1e-06 * length)
-    stores = []
     for b in range(rows // LANES):
         block = pl.ds(b * LANES, LANES)
         by_row = jnp.broadcast_to(scale[b : b + 1], (LANES, LANES)).T
         for g in range(groups):
             at = pl.ds(g * LANES, LANES)
             out[block, at] = (states[g, block] * by_row).astype(BF16)
-        stores.append(pltpu.make_async_copy(out.at[block], out_hbm.at[0, block], out_sem.at[b]))
-        stores[b].start()
-    for store in stores:
-        store.wait()
+        pltpu.make_async_copy(out.at[block], out_hbm.at[0, block], out_sem).start()
+    arrived(out, out_sem)
 
 
 def per_device(fade_rate, update_in, norm_gain):
@@ -383,8 +389,6 @@
             pltpu.VMEM((2, 2, groups, LANES), F32),
             pltpu.VMEM((n_time, 2, groups, LANES), F32),
             pltpu.VMEM((n_chan, rows // LANES, LANES), F32),
-            pltpu.SemaphoreType.DMA((groups,)),
-            pltpu.SemaphoreType.DMA,
             pltpu.SemaphoreType.DMA,
             pltpu.SemaphoreType.DMA((2,)),
             pltpu.SemaphoreType.DMA,
@@ -404,7 +408,7 @@
         out_specs=anywhere,
         scratch_shapes=[
             pltpu.VMEM((rows, columns), BF16),
-            pltpu.SemaphoreType.DMA((rows // LANES,)),
+            pltpu.SemaphoreType.DMA,
         ],
         name="channel_norm",
     )(states, power)

time: 16.7 us -> 16.7 us (level)
  no operation moved by 1% of the time
where the time goes in v8:
time: 16.7 us; the launch traced here: 16.4 us
  Pallas kernels  16.4 us (98%)
    pallas_call x1, Pallas kernels, per_device(): pl.pallas_call(functools.partial(states_kernel, (n_time, n_chan)), out_sh...  15.5 us
    pallas_call x1, Pallas kernels, per_device(): pl.pallas_call(functools.partial(norm_kernel, (columns * n_chan, rows * n...  0.91 us

profile of v8, /device:TPU:0, one launch (start us, length us, event | category | flops | bytes accessed | tf_op | source)
XLA Modules:
  0.0 16.4 jit_solution(14548476232776816482)
XLA Ops:
  0.0 15.5 %filter_states.1 = (f32[4,512,128]{2,1,0:T(8,128)S(1)}, f32[4,128]{1,0:T(4,128)S(1)}) custom-call(f32[1,512,512]{2,1,0:T(8,128)} %fade_hbm.1, bf16[1,512,512]{2,1,0:T(8,128)(2,1)} %update_hbm.1, f32[1,512]{1,0:T(1,128)} %bitcast.1), custom_call_target="tpu_custom_call" | custom-call | tf_op jit(solution)/shard_map/filter_states/pallas_call | solution.py:372
  15.5 0.9 %channel_norm.1 = bf16[1,512,512]{2,1,0:T(8,128)(2,1)} custom-call(f32[4,512,128]{2,1,0:T(8,128)S(1)} %get-tuple-element.7.states, f32[4,128]{1,0:T(4,128)S(1)} %get-tuple-element.8.power), custom_call_target="tpu_custom_call" | custom-call | tf_op jit(solution)/shard_map/channel_norm/pallas_call | solution.py:404

commit v9 on v8

--- a/solution.py
+++ b/solution.py
@@ -368,7 +368,7 @@
     groups = columns // LANES
     anywhere = pl.BlockSpec(memory_space=pl.ANY)
     vmem = pl.BlockSpec(memory_space=pltpu.VMEM)
-    slabs = pltpu.VMEM((PIECES * groups, rows // (PIECES * RUNS) * PITCH, LANES), F32)
+    slabs = pltpu.VMEM((PIECES * groups, rows // (PIECES * RUNS) * PITCH + 32, LANES), F32)
     states, power = pl.pallas_call(
         functools.partial(states_kernel, (n_time, n_chan)),
         out_shape=(

time: 16.7 us -> 16.7 us (level)
  no operation moved by 1% of the time
where the time goes in v9:
time: 16.7 us; the launch traced here: 16.4 us
  Pallas kernels  16.4 us (98%)
    pallas_call x1, Pallas kernels, per_device(): pl.pallas_call(functools.partial(states_kernel, (n_time, n_chan)), out_sh...  15.5 us
    pallas_call x1, Pallas kernels, per_device(): pl.pallas_call(functools.partial(norm_kernel, (columns * n_chan, rows * n...  0.91 us

profile of v9, /device:TPU:0, one launch (start us, length us, event | category | flops | bytes accessed | tf_op | source)
XLA Modules:
  0.0 16.4 jit_solution(12933450987938181104)
XLA Ops:
  0.0 15.5 %filter_states.1 = (f32[4,512,128]{2,1,0:T(8,128)S(1)}, f32[4,128]{1,0:T(4,128)S(1)}) custom-call(f32[1,512,512]{2,1,0:T(8,128)} %fade_hbm.1, bf16[1,512,512]{2,1,0:T(8,128)(2,1)} %update_hbm.1, f32[1,512]{1,0:T(1,128)} %bitcast.1), custom_call_target="tpu_custom_call" | custom-call | tf_op jit(solution)/shard_map/filter_states/pallas_call | solution.py:372
  15.5 0.9 %channel_norm.1 = bf16[1,512,512]{2,1,0:T(8,128)(2,1)} custom-call(f32[4,512,128]{2,1,0:T(8,128)S(1)} %get-tuple-element.7.states, f32[4,128]{1,0:T(4,128)S(1)} %get-tuple-element.8.power), custom_call_target="tpu_custom_call" | custom-call | tf_op jit(solution)/shard_map/channel_norm/pallas_call | solution.py:404

commit v10 on v9

--- a/solution.py
+++ b/solution.py
@@ -353,12 +353,14 @@
     groups, rows, _ = states.shape
     scale = lax.rsqrt(power[...] * (1.0 / channels) + 1e-06 * length)
     for b in range(rows // LANES):
-        block = pl.ds(b * LANES, LANES)
         by_row = jnp.broadcast_to(scale[b : b + 1], (LANES, LANES)).T
-        for g in range(groups):
-            at = pl.ds(g * LANES, LANES)
-            out[block, at] = (states[g, block] * by_row).astype(BF16)
-        pltpu.make_async_copy(out.at[block], out_hbm.at[0, block], out_sem).start()
+        for h in range(2):
+            part = pl.ds(b * LANES + h * (LANES // 2), LANES // 2)
+            for g in range(groups):
+                at = pl.ds(g * LANES, LANES)
+                half = by_row[h * (LANES // 2) : (h + 1) * (LANES // 2)]
+                out[part, at] = (states[g, part] * half).astype(BF16)
+            pltpu.make_async_copy(out.at[part], out_hbm.at[0, part], out_sem).start()
     arrived(out, out_sem)
 
 

time: 16.7 us -> 16.6 us (level)
  no operation moved by 1% of the time
where the time goes in v10:
time: 16.6 us; the launch traced here: 16.4 us
  Pallas kernels  16.4 us (99%)
    pallas_call x1, Pallas kernels, per_device(): pl.pallas_call(functools.partial(states_kernel, (n_time, n_chan)), out_sh...  15.5 us
    pallas_call x1, Pallas kernels, per_device(): pl.pallas_call(functools.partial(norm_kernel, (columns * n_chan, rows * n...  0.88 us

profile of v10, /device:TPU:0, one launch (start us, length us, event | category | flops | bytes accessed | tf_op | source)
XLA Modules:
  0.0 16.4 jit_solution(1640960567993006810)
XLA Ops:
  0.0 15.5 %filter_states.1 = (f32[4,512,128]{2,1,0:T(8,128)S(1)}, f32[4,128]{1,0:T(4,128)S(1)}) custom-call(f32[1,512,512]{2,1,0:T(8,128)} %fade_hbm.1, bf16[1,512,512]{2,1,0:T(8,128)(2,1)} %update_hbm.1, f32[1,512]{1,0:T(1,128)} %bitcast.1), custom_call_target="tpu_custom_call" | custom-call | tf_op jit(solution)/shard_map/filter_states/pallas_call | solution.py:374
  15.5 0.9 %channel_norm.1 = bf16[1,512,512]{2,1,0:T(8,128)(2,1)} custom-call(f32[4,512,128]{2,1,0:T(8,128)S(1)} %get-tuple-element.7.states, f32[4,128]{1,0:T(4,128)S(1)} %get-tuple-element.8.power), custom_call_target="tpu_custom_call" | custom-call | tf_op jit(solution)/shard_map/channel_norm/pallas_call | solution.py:406
